TPU v7x, 32 devices: a whole 2x2x4 slice. The times are simulated.
32 devices in a mesh: row: 4 (over z), col: 8 (over y, x, core).
Axes of the slice: x: 2, y: 2, z: 4, core: 2. Of those that a mesh axis runs over, the one named last changes fastest.
Arguments:
- tokens: bfloat16 [24576, 256], P(('row', 'col'))
- codebook: bfloat16 [16384, 256], P(('row', 'col')), may hold values from -6 to 6
- codes: int32 [24576], P(('row', 'col')), may hold values from 0 to 16383
Outputs:
- quantized: bfloat16 [24576, 256], P(('row', 'col'))
- token_loss: float32 [24576], P(('row', 'col'))
- code_counts: int32 [16384], P(('row', 'col'))
- code_loss: float32 [16384], P(('row', 'col'))
- commitment: float32 [], replicated
- perplexity: float32 [], replicated
All inputs are finite; a program needn't handle non-finite values.
Results may differ from a plain program's by a relative error of at most 0.0004.
Values may be sent and summed in bfloat16 or wider, within the bound.
A program may use at most 64 MiB of HBM per device.

v0:
```python
import functools

import jax
import jax.numpy as jnp
from jax import lax
from jax.experimental import pallas as pl
from jax.experimental.pallas import tpu as pltpu
from jax.sharding import PartitionSpec as P

AXES = ("row", "col")
EXTRA = 128
GROUP = 4
F32 = jnp.float32
BF16 = jnp.bfloat16


def dense_plan(tokens, codebook, codes):
    tok_rows = tokens.shape[0]
    width = tokens.shape[1]
    per_dev = codebook.shape[0]
    devices = lax.axis_size("row") * lax.axis_size("col")
    total_codes = per_dev * devices
    total_tokens = tok_rows * devices
    full_book = lax.all_gather(codebook, AXES, axis=0, tiled=True)
    quantized = jnp.take(full_book, codes, axis=0)
    diff = tokens.astype(F32) - quantized.astype(F32)
    token_loss = jnp.sum(diff * diff, axis=1) / width
    loss_part = jnp.sum(token_loss)
    local_counts = jax.ops.segment_sum(
        jnp.ones((tok_rows,), F32), codes, num_segments=total_codes
    )
    local_loss = jax.ops.segment_sum(token_loss, codes, num_segments=total_codes)
    floor_prob = jnp.float32(1.0 / total_tokens)
    totals, loss_totals = lax.psum((local_counts, local_loss), AXES)
    loss_sum = lax.psum(loss_part, AXES)
    probs = totals / total_tokens
    terms = jnp.where(
        totals > 0.5, probs * jnp.log(jnp.maximum(probs, floor_prob)), jnp.float32(0.0)
    )
    offset = lax.axis_index(AXES) * per_dev
    owned_counts = lax.dynamic_slice_in_dim(totals, offset, per_dev, 0)
    code_loss = lax.dynamic_slice_in_dim(loss_totals, offset, per_dev, 0)
    commitment = 0.25 * loss_sum / total_tokens
    return (
        quantized,
        token_loss,
        owned_counts.astype(jnp.int32),
        code_loss,
        commitment,
        jnp.exp(-jnp.sum(terms)),
    )


def ring_plan(n, tokens, codebook, codes):
    rows, width = tokens.shape
    per_dev = codebook.shape[0]
    me = lax.axis_index(AXES)
    ring = [(i, (i + 1) % n) for i in range(n)]
    hi = codes // per_dev
    lo = codes % per_dev

    def pick(step, carry):
        block, got = carry
        owner = lax.rem(me - step + n, n)
        got = jnp.where((hi == owner)[:, None], jnp.take(block, lo, axis=0), got)
        return lax.ppermute(block, AXES, ring), got

    _, quantized = lax.fori_loop(0, n, pick, (codebook, jnp.zeros_like(tokens)))
    diff = tokens.astype(F32) - quantized.astype(F32)
    token_loss = jnp.sum(diff * diff, axis=1) / width

    def add(step, carry):
        c, t, total, parts = carry
        owner = lax.rem(me - step + n, n)
        mine = (c // per_dev) == me
        total = total + jax.ops.segment_sum(
            jnp.where(mine, t, 0.0), c % per_dev, num_segments=per_dev
        )
        parts = lax.dynamic_update_slice(parts, jnp.sum(t)[None], (owner,))
        return lax.ppermute(c, AXES, ring), lax.ppermute(t, AXES, ring), total, parts

    start = (codes, token_loss, jnp.zeros((per_dev,), F32), jnp.zeros((n,), F32))
    _, _, code_loss, parts = lax.fori_loop(0, n, add, start)
    return quantized, token_loss, code_loss, 0.25 * jnp.sum(parts) / (rows * n)


def kernel(
    n, cols, cap, order_of,
    codes_ref, tokens_ref, book_ref,
    quant_ref, tloss_ref, counts_ref, closs_ref, commit_ref, perp_ref, flag_ref,
    csend, crecv, psend, precv, lsend, lrecv, ranks, low1h, sel,
    csem_s, csem_r, psem_s, psem_r, lsem_s, lsem_r,
):
    rows, width = tokens_ref.shape
    per = book_ref.shape[0]
    bits = per.bit_length() - 1
    total_tokens = rows * n
    my_row, my_col = lax.axis_index("row"), lax.axis_index("col")
    me = my_row * cols + my_col
    rows_at = [lax.rem(my_row + d, n // cols) for d in range(n // cols)]
    cols_at = [lax.rem(my_col + d, cols) for d in range(cols)]
    at = [(rows_at[k // cols], cols_at[k % cols]) for k in range(n)]
    peer = [r * cols + c for r, c in at]

    def copy(send, recv, ssem, rsem, k):
        return pltpu.make_async_remote_copy(
            src_ref=send.at[peer[k]],
            dst_ref=recv.at[me],
            send_sem=ssem.at[k],
            recv_sem=rsem.at[k],
            device_id=at[k],
            device_id_type=pl.DeviceIdType.MESH,
        )

    def start_all(*refs):
        for k in order_of:
            if k:
                copy(*refs, k).start()

    def wait_all(*refs):
        for k in order_of:
            if k:
                copy(*refs, k).wait_recv()

    def sent_all(*refs):
        for k in order_of:
            if k:
                copy(*refs, k).wait_send()

    barrier = pltpu.get_barrier_semaphore()
    for k in order_of:
        if k:
            pl.semaphore_signal(
                barrier, inc=1, device_id=at[k], device_id_type=pl.DeviceIdType.MESH
            )

    code_row = codes_ref[...]
    hi_row = lax.shift_right_logical(code_row, bits)
    code_col = jnp.broadcast_to(code_row.astype(F32), (128, rows)).T.astype(jnp.int32)
    hi_col = lax.shift_right_logical(code_col, bits)
    lo_col = code_col & (per - 1)
    lane = lax.broadcasted_iota(jnp.int32, (rows, 128), 1)
    own_row = hi_row == lax.broadcasted_iota(jnp.int32, (n, rows), 0)
    for k in range(per // 128):
        low1h[:, k * 128 : (k + 1) * 128] = jnp.where(lo_col == lane + k * 128, 1.0, 0.0).astype(BF16)
    low = low1h[...]
    hist = jnp.dot(jnp.where(own_row, 1.0, 0.0).astype(BF16), low, preferred_element_type=F32)
    wanted = jnp.where(hist > 0.5, 1.0, 0.0)
    most = jnp.max(jnp.sum(wanted, axis=1, keepdims=True), axis=0, keepdims=True)
    most_wide = jnp.broadcast_to(most, (1, EXTRA))
    for p in range(n):
        csend[p, :, :per] = hist[p : p + 1, :]
        csend[p, :, per:] = most_wide
    crecv[pl.ds(me, 1)] = csend[pl.ds(me, 1)]

    pl.semaphore_wait(barrier, n - 1)
    start_all(csend, crecv, csem_s, csem_r)

    before = lax.broadcasted_iota(jnp.int32, (per, per), 0) < lax.broadcasted_iota(jnp.int32, (per, per), 1)
    before = jnp.where(before, 1.0, 0.0).astype(BF16)
    rank = jnp.dot(wanted.astype(BF16), before, preferred_element_type=F32)
    rank = jnp.minimum(rank, 255.0).astype(BF16)
    hi1h = jnp.where(hi_col[:, :n] == lane[:, :n], 1.0, 0.0).astype(BF16)
    looked = jnp.dot(hi1h, rank, preferred_element_type=F32).astype(BF16) * low
    found = jnp.dot(looked, jnp.ones((per, 128), BF16), preferred_element_type=F32)
    slot = hi_col * cap + found.astype(jnp.int32)
    for k in range(n * cap // 128):
        sel[:, k * 128 : (k + 1) * 128] = jnp.where(slot == lane + k * 128, 1.0, 0.0).astype(BF16)

    wait_all(csend, crecv, csem_s, csem_r)
    asked = crecv[:, 0, :per]
    present = asked > 0.5
    order = jnp.dot(jnp.where(present, 1.0, 0.0).astype(BF16), before, preferred_element_type=F32)
    order = jnp.where(present, order, -1.0)
    for p in range(n):
        ranks[p] = order[p : p + 1, :]

    place = lax.broadcasted_iota(jnp.int32, (cap, per), 0).astype(F32)
    book = book_ref[...]
    ready = []
    for g in range(0, n, GROUP):
        group = order_of[g : g + GROUP]
        picks = [
            jnp.where(jnp.broadcast_to(ranks[peer[k]], (cap, per)) == place, 1.0, 0.0).astype(BF16)
            for k in group
        ]
        packed = jnp.dot(jnp.concatenate(picks, axis=0), book, preferred_element_type=F32)
        packed = packed.astype(BF16)
        for i, k in enumerate(group):
            out = psend if k else precv
            out[peer[k]] = packed[i * cap : (i + 1) * cap]
        for k in ready:
            copy(psend, precv, psem_s, psem_r, k).start()
        ready = [k for k in group if k]
    for k in ready:
        copy(psend, precv, psem_s, psem_r, k).start()

    counts = jnp.sum(asked, axis=0, keepdims=True)
    counts_ref[...] = counts.astype(jnp.int32)
    probs = counts / total_tokens
    terms = jnp.where(
        counts > 0.5, probs * jnp.log(jnp.maximum(probs, 1.0 / total_tokens)), 0.0
    )
    entropy = jnp.sum(terms, axis=1, keepdims=True)
    flag_ref[0, 0] = jnp.max(crecv[:, 0, per:]).astype(jnp.int32)

    wait_all(psend, precv, psem_s, psem_r)
    packs = precv[...].reshape(n * cap, width)
    quant = jnp.dot(sel[...], packs, preferred_element_type=F32).astype(BF16)
    quant_ref[...] = quant
    diff = tokens_ref[...].astype(F32) - quant.astype(F32)
    square = diff * diff
    folded = square[:, :128]
    for k in range(1, width // 128):
        folded = folded + square[:, k * 128 : (k + 1) * 128]
    tloss = jnp.sum(folded.T, axis=0, keepdims=True) / width
    tloss_ref[...] = tloss
    part = jnp.sum(tloss, axis=1, keepdims=True)

    first = tloss.astype(BF16).astype(F32)
    second = (tloss - first).astype(BF16).astype(F32)
    third = tloss - first - second
    spread = jnp.concatenate(
        [jnp.where(own_row, x, 0.0).astype(BF16) for x in (first, second, third)], axis=0
    )
    sums = jnp.dot(spread, low1h[...], preferred_element_type=F32)
    sums = sums[:n] + sums[n : 2 * n] + sums[2 * n :]
    lane1 = lax.broadcasted_iota(jnp.int32, (1, EXTRA), 1)
    tail = jnp.where(lane1 == 0, part, jnp.where(lane1 == 1, entropy, 0.0))
    for p in range(n):
        lsend[p, :, :per] = sums[p : p + 1, :]
        lsend[p, :, per:] = tail
    lrecv[pl.ds(me, 1)] = lsend[pl.ds(me, 1)]
    start_all(lsend, lrecv, lsem_s, lsem_r)

    sent_all(csend, crecv, csem_s, csem_r)
    sent_all(psend, precv, psem_s, psem_r)
    wait_all(lsend, lrecv, lsem_s, lsem_r)
    added = jnp.sum(lrecv[:, 0, :], axis=0, keepdims=True)
    closs_ref[...] = added[:, :per]
    ends = added[:, per:]
    commit_ref[0, 0] = jnp.sum(jnp.where(lane1 == 0, ends, 0.0)) * (0.25 / total_tokens)
    perp = jnp.exp(-jnp.sum(jnp.where(lane1 == 1, ends, 0.0), axis=1, keepdims=True))
    perp_ref[0, 0] = jnp.max(jnp.broadcast_to(perp, (1, EXTRA)))
    sent_all(lsend, lrecv, lsem_s, lsem_r)


def send_order(n, cols):
    turns = sorted(range(n // cols), key=lambda d: (abs(2 * d - n // cols), d))
    turns = [d for d in turns if d] + [0]
    blocks = [(d, h) for d in turns for h in (0, 1)]
    half = cols // 2
    spread = sorted(blocks[2:-2], key=lambda b: b[1])
    blocks = blocks[:2] + spread + [(0, 1), (0, 0)]
    return [d * cols + h * half + c for d, h in blocks for c in range(half)]


def exchange(n, cols, cap, number, tokens, codebook, codes):
    rows, width = tokens.shape
    per = codebook.shape[0]
    vmem = pl.BlockSpec(memory_space=pltpu.VMEM)
    smem = pl.BlockSpec(memory_space=pltpu.SMEM)
    dma = pltpu.SemaphoreType.DMA((n,))
    message = pltpu.VMEM((n, 1, per + EXTRA), F32)
    return pl.pallas_call(
        functools.partial(kernel, n, cols, cap, send_order(n, cols)),
        out_shape=(
            jax.ShapeDtypeStruct((rows, width), BF16),
            jax.ShapeDtypeStruct((1, rows), F32),
            jax.ShapeDtypeStruct((1, per), jnp.int32),
            jax.ShapeDtypeStruct((1, per), F32),
            jax.ShapeDtypeStruct((1, 1), F32),
            jax.ShapeDtypeStruct((1, 1), F32),
            jax.ShapeDtypeStruct((1, 1), jnp.int32),
        ),
        in_specs=[vmem] * 3,
        out_specs=(vmem, vmem, vmem, vmem, smem, smem, smem),
        scratch_shapes=[
            message, message,
            pltpu.VMEM((n, cap, width), BF16),
            pltpu.VMEM((n, cap, width), BF16),
            message, message,
            pltpu.VMEM((n, 1, per), F32),
            pltpu.VMEM((rows, per), BF16),
            pltpu.VMEM((rows, n * cap), BF16),
            dma, dma, dma, dma, dma, dma,
        ],
        compiler_params=pltpu.CompilerParams(collective_id=number, has_side_effects=True),
    )(codes, tokens, codebook)


def asked_plan(n, cols, cap, tokens, codebook, codes):
    rows = tokens.shape[0]
    per = codebook.shape[0]
    code_row = codes.reshape(1, rows)
    quantized, token_loss, counts, code_loss, commitment, perplexity, flag = exchange(
        n, cols, cap, 0, tokens, codebook, code_row
    )

    def kept():
        return quantized, token_loss.reshape(rows), code_loss.reshape(per), commitment[0, 0]

    def wider():
        q, t, _, c, m, _, _ = exchange(n, cols, 2 * cap, 1, tokens, codebook, code_row)
        return q, t.reshape(rows), c.reshape(per), m[0, 0]

    def any_codes():
        return lax.cond(
            flag[0, 0] > 2 * cap, lambda: ring_plan(n, tokens, codebook, codes), wider
        )

    quantized, token_loss, code_loss, commitment = lax.cond(flag[0, 0] > cap, any_codes, kept)
    return (
        quantized,
        token_loss,
        counts.reshape(per),
        code_loss,
        commitment,
        perplexity[0, 0],
    )


def on_device(n, cols, tokens, codebook, codes):
    rows, width = tokens.shape
    per = codebook.shape[0]
    cap = -(-rows // (n * 16)) * 16
    fits = (
        per % 128 == 0
        and per & (per - 1) == 0
        and rows % 128 == 0
        and width % 128 == 0
        and n * cap % 128 == 0
        and cols % 8 == 0
        and n // cols > 1
        and n <= 128
        and 2 * cap < min(per, 256)
    )
    if fits:
        return asked_plan(n, cols, cap, tokens, codebook, codes)
    return dense_plan(tokens, codebook, codes)


def solution(mesh):
    n = mesh.shape["row"] * mesh.shape["col"]
    return jax.shard_map(
        functools.partial(on_device, n, mesh.shape["col"]),
        mesh=mesh,
        in_specs=(P(AXES, None), P(AXES, None), P(AXES)),
        out_specs=(P(AXES, None), P(AXES), P(AXES), P(AXES), P(), P()),
        check_vma=False,
    )
```

profile of v0, /device:TPU:0, one launch (start us, length us, event | category | flops | bytes accessed | tf_op | source)
XLA Modules:
  0.0 44.2 jit_solution(15242491422312314159)
XLA Ops:
  0.6 0.0 copy-start
  0.6 0.7 %copy.61 = s32[768]{0:T(1024)S(1)} copy(s32[768]{0:T(1024)} %param.13) | data formatting | bytes 6144
  1.4 0.9 %copy.60.book_ref = bf16[512,256]{1,0:T(8,128)(2,1)S(1)} copy(bf16[512,256]{1,0:T(8,128)(2,1)} %param.12) | data formatting | bytes 524288
  2.3 0.0 copy-done
  2.3 33.3 %shard_map.82 = (bf16[768,256]{1,0:T(8,128)(2,1)}, f32[1,768]{1,0:T(1,128)S(1)}, s32[1,512]{1,0:T(1,128)}, f32[1,512]{1,0:T(1,128)}, f32[1,1]{1,0:T(1,128)}, /*index=5*/f32[1,1]{1,0:T(1,128)}, s32[1,1]{1,0:T(1,128)}) custom-call(s32[1,768]{1,0:T(1,128)S(1)} %reshape.65.codes_ref, bf16[768,256]{1,0:T(8,128)(2,1)S(1)} %copy-done, ...), custom_call_target="tpu_custom_call" | custom-call | tf_op jit(solution)/shard_map/pallas_call | solution.py:265
  36.4 0.6 %conditional.2 = ((bf16[768,256]{1,0:T(8,128)(2,1)}, f32[768]{0:T(1024)}, f32[512]{0:T(512)}, f32[]{:T(128)})) conditional(s32[]{:T(128)} %bitcast.6, (f32[1,768]{1,0:T(1,128)S(1)}, f32[1,512]{1,0:T(1,128)}, f32[1,1]{1,0:T(1,128)}, bf16[768,256]{1,0:T(8,128)(2,1)}) %tuple.99, (s32[1,1]{1,0:T(1,128)}, s32[1,768]{1,0:T(1,128)S(1)}, ...), branch_computations={%region_0.0_spmd, %region_1.12_spmd} | conditional | flops 1619264 | bytes 4443314 | solution.py:312
  36.4 0.6 %reduce = f32[768]{0:T(1024)} reduce(f32[1,768]{1,0:T(1,128)S(1)} %get-tuple-element.281, f32[]{:T(128)} %constant.216), dimensions={0}, to_apply=%get-tuple-element.281.reduce_sub_computation | reduce | bytes 6148 | tf_op jit(solution)/shard_map
  37.0 0.0 copy-start.2
  37.0 1.8 %copy.62 = bf16[768,256]{1,0:T(8,128)(2,1)} copy(bf16[768,256]{1,0:T(8,128)(2,1)} %get-tuple-element.563) | data formatting | bytes 786432
  38.8 0.0 copy-done.2
  38.8 0.6 %copy.63 = s32[512]{0:T(512)} copy(s32[512]{0:T(512)S(1)} %bitcast.11) | data formatting | bytes 4096
  39.3 1.3 %copy.64 = f32[512]{0:T(512)} copy(f32[512]{0:T(512)} %get-tuple-element.566) | data formatting | bytes 4096
  (1 shorter events, 0.0 us)
Async XLA Ops:
  0.6 1.7 %copy-start = (bf16[768,256]{1,0:T(8,128)(2,1)S(1)}, bf16[768,256]{1,0:T(8,128)(2,1)}, u32[]{:S(2)}) copy-start(bf16[768,256]{1,0:T(8,128)(2,1)} %tokens_ref.1) | copy-start | bytes 1179652
  37.0 1.8 %copy-start.2 = (s32[1,512]{1,0:T(1,128)S(1)}, s32[1,512]{1,0:T(1,128)}, u32[]{:S(2)}) copy-start(s32[1,512]{1,0:T(1,128)} %get-tuple-element.340) | copy-start | bytes 6148
where the time goes:
time: 44.4 us; the launch traced here: 44.2 us
  Pallas kernels  33.3 us (75%)
  local copies, waits for them, and re-layouts  5.3 us (12%)
  between operations  4.9 us (11%)
  other arithmetic  0.61 us (1%)
    pallas_call x1, Pallas kernels, exchange(): pl.pallas_call(functools.partial(kernel, n, cols, cap, send_order(n, cols...  33.3 us
    unnamed x9, local copies, waits for them, and re-layouts  5.3 us

commit v1 on v0

--- a/solution.py
+++ b/solution.py
@@ -56,6 +56,8 @@
     per_dev = codebook.shape[0]
     me = lax.axis_index(AXES)
     ring = [(i, (i + 1) % n) for i in range(n)]
+    codes = jnp.where(me < n, codes, 0)
+    codebook = jnp.where(me < n, codebook, 0)
     hi = codes // per_dev
     lo = codes % per_dev
 
@@ -70,29 +72,52 @@
     token_loss = jnp.sum(diff * diff, axis=1) / width
 
     def add(step, carry):
-        c, t, total, parts = carry
+        c, t, total, hits, parts = carry
         owner = lax.rem(me - step + n, n)
         mine = (c // per_dev) == me
         total = total + jax.ops.segment_sum(
             jnp.where(mine, t, 0.0), c % per_dev, num_segments=per_dev
         )
+        hits = hits + jax.ops.segment_sum(
+            mine.astype(jnp.int32), c % per_dev, num_segments=per_dev
+        )
         parts = lax.dynamic_update_slice(parts, jnp.sum(t)[None], (owner,))
-        return lax.ppermute(c, AXES, ring), lax.ppermute(t, AXES, ring), total, parts
-
-    start = (codes, token_loss, jnp.zeros((per_dev,), F32), jnp.zeros((n,), F32))
-    _, _, code_loss, parts = lax.fori_loop(0, n, add, start)
-    return quantized, token_loss, code_loss, 0.25 * jnp.sum(parts) / (rows * n)
+        return lax.ppermute(c, AXES, ring), lax.ppermute(t, AXES, ring), total, hits, parts
+
+    start = (
+        codes, token_loss, jnp.zeros((per_dev,), F32),
+        jnp.zeros((per_dev,), jnp.int32), jnp.zeros((n,), F32),
+    )
+    _, _, code_loss, counts, parts = lax.fori_loop(0, n, add, start)
+    probs = counts.astype(F32) / (rows * n)
+    floor_prob = jnp.float32(1.0 / (rows * n))
+    terms = jnp.where(counts > 0, probs * jnp.log(jnp.maximum(probs, floor_prob)), 0.0)
+
+    def collect(step, carry):
+        entropy, parts = carry
+        owner = lax.rem(me - step + n, n)
+        parts = lax.dynamic_update_slice(parts, entropy, (owner,))
+        return lax.ppermute(entropy, AXES, ring), parts
+
+    _, entropies = lax.fori_loop(0, n, collect, (jnp.sum(terms)[None], jnp.zeros((n,), F32)))
+    commitment = 0.25 * jnp.sum(parts) / (rows * n)
+    return quantized, token_loss, counts, code_loss, commitment, jnp.exp(-jnp.sum(entropies))
 
 
 def kernel(
     n, cols, cap, order_of,
-    codes_ref, tokens_ref, book_ref,
+    codes_hbm, tokens_hbm, book_hbm,
     quant_ref, tloss_ref, counts_ref, closs_ref, commit_ref, perp_ref, flag_ref,
+    codes_ref, tokens_ref, book_ref, in_sem,
     csend, crecv, psend, precv, lsend, lrecv, ranks, low1h, sel,
     csem_s, csem_r, psem_s, psem_r, lsem_s, lsem_r,
 ):
-    rows, width = tokens_ref.shape
-    per = book_ref.shape[0]
+    rows, width = tokens_hbm.shape
+    per = book_hbm.shape[0]
+    fetch_codes = pltpu.make_async_copy(codes_hbm, codes_ref, in_sem.at[0])
+    fetch_book = pltpu.make_async_copy(book_hbm, book_ref, in_sem.at[1])
+    fetch_tokens = pltpu.make_async_copy(tokens_hbm, tokens_ref, in_sem.at[2])
+    fetch_codes.start()
     bits = per.bit_length() - 1
     total_tokens = rows * n
     my_row, my_col = lax.axis_index("row"), lax.axis_index("col")
@@ -133,8 +158,11 @@
             pl.semaphore_signal(
                 barrier, inc=1, device_id=at[k], device_id_type=pl.DeviceIdType.MESH
             )
-
-    code_row = codes_ref[...]
+    fetch_book.start()
+    fetch_tokens.start()
+
+    fetch_codes.wait()
+    code_row = codes_ref[...].reshape(1, rows)
     hi_row = lax.shift_right_logical(code_row, bits)
     code_col = jnp.broadcast_to(code_row.astype(F32), (128, rows)).T.astype(jnp.int32)
     hi_col = lax.shift_right_logical(code_col, bits)
@@ -176,6 +204,7 @@
         ranks[p] = order[p : p + 1, :]
 
     place = lax.broadcasted_iota(jnp.int32, (cap, per), 0).astype(F32)
+    fetch_book.wait()
     book = book_ref[...]
     ready = []
     for g in range(0, n, GROUP):
@@ -205,6 +234,7 @@
     flag_ref[0, 0] = jnp.max(crecv[:, 0, per:]).astype(jnp.int32)
 
     wait_all(psend, precv, psem_s, psem_r)
+    fetch_tokens.wait()
     packs = precv[...].reshape(n * cap, width)
     quant = jnp.dot(sel[...], packs, preferred_element_type=F32).astype(BF16)
     quant_ref[...] = quant
@@ -273,9 +303,13 @@
             jax.ShapeDtypeStruct((1, 1), F32),
             jax.ShapeDtypeStruct((1, 1), jnp.int32),
         ),
-        in_specs=[vmem] * 3,
+        in_specs=[pl.BlockSpec(memory_space=pltpu.HBM)] * 3,
         out_specs=(vmem, vmem, vmem, vmem, smem, smem, smem),
         scratch_shapes=[
+            pltpu.VMEM(codes.shape, jnp.int32),
+            pltpu.VMEM((rows, width), BF16),
+            pltpu.VMEM((per, width), BF16),
+            pltpu.SemaphoreType.DMA((3,)),
             message, message,
             pltpu.VMEM((n, cap, width), BF16),
             pltpu.VMEM((n, cap, width), BF16),
@@ -286,38 +320,66 @@
             dma, dma, dma, dma, dma, dma,
         ],
         compiler_params=pltpu.CompilerParams(collective_id=number, has_side_effects=True),
-    )(codes, tokens, codebook)
+    )(*[pltpu.with_memory_space_constraint(x, pltpu.HBM) for x in (codes, tokens, codebook)])
+
+
+def finish_kernel(
+    quant_ref, tloss_ref, counts_ref, closs_ref, commit_ref, perp_ref,
+    quant_out, tloss_out, counts_out, closs_out, commit_out, perp_out, sem,
+):
+    put = pltpu.make_async_copy(quant_ref, quant_out, sem)
+    put.start()
+    tloss_out[...] = tloss_ref[...].reshape(tloss_out.shape)
+    counts_out[...] = counts_ref[...].reshape(counts_out.shape)
+    closs_out[...] = closs_ref[...].reshape(closs_out.shape)
+    commit_out[0, 0] = commit_ref[0, 0]
+    perp_out[0, 0] = perp_ref[0, 0]
+    put.wait()
+
+
+def finish(quantized, token_loss, counts, code_loss, commitment, perplexity):
+    rows, per = token_loss.shape[1], counts.shape[1]
+    vmem = pl.BlockSpec(memory_space=pltpu.VMEM)
+    smem = pl.BlockSpec(memory_space=pltpu.SMEM)
+    q, t, k, c, m, p = pl.pallas_call(
+        finish_kernel,
+        out_shape=(
+            jax.ShapeDtypeStruct(quantized.shape, BF16),
+            jax.ShapeDtypeStruct((rows,), F32),
+            jax.ShapeDtypeStruct((per,), jnp.int32),
+            jax.ShapeDtypeStruct((per,), F32),
+            jax.ShapeDtypeStruct((1, 1), F32),
+            jax.ShapeDtypeStruct((1, 1), F32),
+        ),
+        in_specs=[vmem] * 4 + [smem] * 2,
+        out_specs=(pl.BlockSpec(memory_space=pltpu.HBM), vmem, vmem, vmem, smem, smem),
+        scratch_shapes=[pltpu.SemaphoreType.DMA],
+    )(quantized, token_loss, counts, code_loss, commitment, perplexity)
+    return q, t, k, c, m[0, 0], p[0, 0]
 
 
 def asked_plan(n, cols, cap, tokens, codebook, codes):
     rows = tokens.shape[0]
     per = codebook.shape[0]
-    code_row = codes.reshape(1, rows)
+    code_row = codes
     quantized, token_loss, counts, code_loss, commitment, perplexity, flag = exchange(
         n, cols, cap, 0, tokens, codebook, code_row
     )
 
     def kept():
-        return quantized, token_loss.reshape(rows), code_loss.reshape(per), commitment[0, 0]
+        return finish(quantized, token_loss, counts, code_loss, commitment, perplexity)
 
     def wider():
-        q, t, _, c, m, _, _ = exchange(n, cols, 2 * cap, 1, tokens, codebook, code_row)
-        return q, t.reshape(rows), c.reshape(per), m[0, 0]
+        out = exchange(n, cols, 2 * cap, 1, tokens, codebook, code_row)
+        return finish(*out[:6])
+
+    def ringed():
+        return ring_plan(n, tokens, codebook, codes)
 
     def any_codes():
-        return lax.cond(
-            flag[0, 0] > 2 * cap, lambda: ring_plan(n, tokens, codebook, codes), wider
-        )
-
-    quantized, token_loss, code_loss, commitment = lax.cond(flag[0, 0] > cap, any_codes, kept)
-    return (
-        quantized,
-        token_loss,
-        counts.reshape(per),
-        code_loss,
-        commitment,
-        perplexity[0, 0],
-    )
+        return lax.cond(flag[0, 0] > 2 * cap, ringed, wider)
+
+    return lax.cond(flag[0, 0] > cap, any_codes, kept)
 
 
 def on_device(n, cols, tokens, codebook, codes):

time: 44.4 us -> 37.7 us (0.85)
  local copies, waits for them, and re-layouts: 5.3 us -> 0.03 us
  between operations: 4.9 us -> 1.51 us
  Pallas kernels: 33.3 us -> 35.7 us
  other arithmetic: 0.61 us -> 0 us
    unnamed x9 -> x6, local copies, waits for them, and re-layouts: 5.3 us -> 0.03 us
    pallas_call x0 -> x1, Pallas kernels: none -> 2.57 us  [finish(): pl.pallas_call(finish_kernel, out_shape=(jax.ShapeDtypeStruct(quantized.s...]
    another operation x1 -> x0, other arithmetic: 0.61 us -> none
where the time goes in v1:
time: 37.7 us; the launch traced here: 37.5 us
  Pallas kernels  35.7 us (95%)
  between operations  1.51 us (4%)
    pallas_call x1, Pallas kernels, exchange(): pl.pallas_call(functools.partial(kernel, n, cols, cap, send_order(n, cols...  33.2 us
    pallas_call x1, Pallas kernels, finish(): pl.pallas_call(finish_kernel, out_shape=(jax.ShapeDtypeStruct(quantized.s...  2.57 us

profile of v1, /device:TPU:0, one launch (start us, length us, event | category | flops | bytes accessed | tf_op | source)
XLA Modules:
  0.0 37.5 jit_solution(17729566012209022762)
XLA Ops:
  0.6 0.0 copy-start
  0.6 0.0 copy-start.2
  0.7 33.2 %shard_map.86 = (bf16[768,256]{1,0:T(8,128)(2,1)S(1)}, f32[1,768]{1,0:T(1,128)S(1)}, s32[1,512]{1,0:T(1,128)S(1)}, f32[1,512]{1,0:T(1,128)S(1)}, f32[1,1]{1,0:T(1,128)}, /*index=5*/f32[1,1]{1,0:T(1,128)}, s32[1,1]{1,0:T(1,128)}) custom-call(s32[768]{0:T(1024)} %codes_hbm.1, bf16[768,256]{1,0:T(8,128)(2,1)} %tokens_hbm.1, bf16[512,256]{1,0:T(8,128)(2,1)} %book_hbm.1), custom_call_target="tpu_custom_call" | custom-call | tf_op jit(solution)/shard_map/pallas_call | solution.py:295
  33.8 0.0 copy-start.4
  34.5 0.0 copy-done
  34.5 0.0 copy-done.2
  34.5 0.0 copy-done.4
  34.5 2.8 %conditional.2 = ((bf16[768,256]{1,0:T(8,128)(2,1)}, f32[768]{0:T(1024)}, s32[512]{0:T(512)}, f32[512]{0:T(512)}, f32[]{:T(128)}, /*index=5*/f32[]{:T(128)})) conditional(s32[]{:T(128)} %bitcast.7, (bf16[768,256]{1,0:T(8,128)(2,1)S(1)}, f32[1,768]{1,0:T(1,128)S(1)}, s32[1,512]{1,0:T(1,128)S(1)}, f32[1,512]{1,0:T(1,128)S(1)}, f32[1,1]{1,0:T(1,128)}, ...), branch_computations={%region_0.0_spmd, %region_1.17_spmd} | conditional | flops 1761645 | bytes 4995427 | solution.py:382
  34.5 2.6 %branch_0_fun.3 = (bf16[768,256]{1,0:T(8,128)(2,1)}, f32[768]{0:T(1024)}, s32[512]{0:T(512)}, f32[512]{0:T(512)}, f32[1,1]{1,0:T(1,128)}, /*index=5*/f32[1,1]{1,0:T(1,128)}) custom-call(bf16[768,256]{1,0:T(8,128)(2,1)S(1)} %get-tuple-element.376.quant_ref, f32[1,768]{1,0:T(1,128)S(1)} %get-tuple-element.377.tloss_ref, ...), custom_call_target="tpu_custom_call" | custom-call | tf_op jit(solution)/shard_map/cond/branch_0_fun/pallas_call | solution.py:344
Async XLA Ops:
  0.6 33.9 %copy-start = (bf16[768,256]{1,0:T(8,128)(2,1)S(1)}, bf16[768,256]{1,0:T(8,128)(2,1)}, u32[]{:S(2)}) copy-start(bf16[768,256]{1,0:T(8,128)(2,1)} %tokens_hbm.1) | copy-start | bytes 1179652
  0.6 33.9 %copy-start.2 = (bf16[512,256]{1,0:T(8,128)(2,1)S(1)}, bf16[512,256]{1,0:T(8,128)(2,1)}, u32[]{:S(2)}) copy-start(bf16[512,256]{1,0:T(8,128)(2,1)} %book_hbm.1) | copy-start | bytes 786436
  33.8 0.7 %copy-start.4 = (s32[768]{0:T(1024)S(1)}, s32[768]{0:T(1024)}, u32[]{:S(2)}) copy-start(s32[768]{0:T(1024)} %codes_hbm.1) | copy-start | bytes 9220

commit v2 on v1

v2 whole, which is shorter than its diff:
```python
import functools

import jax
import jax.numpy as jnp
from jax import lax
from jax.experimental import pallas as pl
from jax.experimental.pallas import tpu as pltpu
from jax.sharding import PartitionSpec as P

AXES = ("row", "col")
EXTRA = 128
GROUP = 4
F32 = jnp.float32
BF16 = jnp.bfloat16


def dense_plan(tokens, codebook, codes):
    tok_rows = tokens.shape[0]
    width = tokens.shape[1]
    per_dev = codebook.shape[0]
    devices = lax.axis_size("row") * lax.axis_size("col")
    total_codes = per_dev * devices
    total_tokens = tok_rows * devices
    full_book = lax.all_gather(codebook, AXES, axis=0, tiled=True)
    quantized = jnp.take(full_book, codes, axis=0)
    diff = tokens.astype(F32) - quantized.astype(F32)
    token_loss = jnp.sum(diff * diff, axis=1) / width
    loss_part = jnp.sum(token_loss)
    local_counts = jax.ops.segment_sum(
        jnp.ones((tok_rows,), F32), codes, num_segments=total_codes
    )
    local_loss = jax.ops.segment_sum(token_loss, codes, num_segments=total_codes)
    floor_prob = jnp.float32(1.0 / total_tokens)
    totals, loss_totals = lax.psum((local_counts, local_loss), AXES)
    loss_sum = lax.psum(loss_part, AXES)
    probs = totals / total_tokens
    terms = jnp.where(
        totals > 0.5, probs * jnp.log(jnp.maximum(probs, floor_prob)), jnp.float32(0.0)
    )
    offset = lax.axis_index(AXES) * per_dev
    owned_counts = lax.dynamic_slice_in_dim(totals, offset, per_dev, 0)
    code_loss = lax.dynamic_slice_in_dim(loss_totals, offset, per_dev, 0)
    commitment = 0.25 * loss_sum / total_tokens
    return (
        quantized,
        token_loss,
        owned_counts.astype(jnp.int32),
        code_loss,
        commitment,
        jnp.exp(-jnp.sum(terms)),
    )


def ring_plan(n, tokens, codebook, codes):
    rows, width = tokens.shape
    per_dev = codebook.shape[0]
    me = lax.axis_index(AXES)
    ring = [(i, (i + 1) % n) for i in range(n)]
    codes = jnp.where(me < n, codes, 0)
    codebook = jnp.where(me < n, codebook, 0)
    hi = codes // per_dev
    lo = codes % per_dev

    def pick(step, carry):
        block, got = carry
        owner = lax.rem(me - step + n, n)
        got = jnp.where((hi == owner)[:, None], jnp.take(block, lo, axis=0), got)
        return lax.ppermute(block, AXES, ring), got

    _, quantized = lax.fori_loop(0, n, pick, (codebook, jnp.zeros_like(tokens)))
    diff = tokens.astype(F32) - quantized.astype(F32)
    token_loss = jnp.sum(diff * diff, axis=1) / width

    def add(step, carry):
        c, t, total, hits, parts = carry
        owner = lax.rem(me - step + n, n)
        mine = (c // per_dev) == me
        total = total + jax.ops.segment_sum(
            jnp.where(mine, t, 0.0), c % per_dev, num_segments=per_dev
        )
        hits = hits + jax.ops.segment_sum(
            mine.astype(jnp.int32), c % per_dev, num_segments=per_dev
        )
        parts = lax.dynamic_update_slice(parts, jnp.sum(t)[None], (owner,))
        return lax.ppermute(c, AXES, ring), lax.ppermute(t, AXES, ring), total, hits, parts

    start = (
        codes, token_loss, jnp.zeros((per_dev,), F32),
        jnp.zeros((per_dev,), jnp.int32), jnp.zeros((n,), F32),
    )
    _, _, code_loss, counts, parts = lax.fori_loop(0, n, add, start)
    probs = counts.astype(F32) / (rows * n)
    floor_prob = jnp.float32(1.0 / (rows * n))
    terms = jnp.where(counts > 0, probs * jnp.log(jnp.maximum(probs, floor_prob)), 0.0)

    def collect(step, carry):
        entropy, parts = carry
        owner = lax.rem(me - step + n, n)
        parts = lax.dynamic_update_slice(parts, entropy, (owner,))
        return lax.ppermute(entropy, AXES, ring), parts

    _, entropies = lax.fori_loop(0, n, collect, (jnp.sum(terms)[None], jnp.zeros((n,), F32)))
    commitment = 0.25 * jnp.sum(parts) / (rows * n)
    return quantized, token_loss, counts, code_loss, commitment, jnp.exp(-jnp.sum(entropies))


def kernel(
    n, cols, cap, order_of,
    codes_hbm, tokens_hbm, book_hbm,
    quant_ref, tloss_ref, counts_ref, closs_ref, scal_ref, flag_ref,
    codes_ref, tokens_ref, book_ref, csend, crecv, psend, precv, dsend, drecv, lsend, lrecv,
    ranks, low1h, sel, rank1h,
    in_sem, csem_s, csem_r, psem_s, psem_r, lsem_s, lsem_r, bsem, dsem,
):
    rows, width = tokens_hbm.shape
    per = book_hbm.shape[0]
    bits = per.bit_length() - 1
    total_tokens = rows * n
    chips, half = n // 2, cols // 2
    my_row, my_col = lax.axis_index("row"), lax.axis_index("col")
    core = lax.rem(my_col, 2)
    my_chip = lax.div(my_col, 2)
    me = my_row * half + my_chip
    rows_at = [lax.rem(my_row + d, chips // half) for d in range(chips // half)]
    chips_at = [lax.rem(my_chip + d, half) for d in range(half)]
    spots = [(rows_at[k // half], chips_at[k % half]) for k in range(chips)]
    at = [(r, 2 * c + core) for r, c in spots]
    mirror = [(r, 2 * c + 1 - core) for r, c in spots]
    peer = [r * half + c for r, c in spots]
    fetch_codes = pltpu.make_async_copy(codes_hbm, codes_ref, in_sem.at[0])
    own_book = book_ref.at[pl.ds(pl.multiple_of(core * per, per), per)]
    fetch_book = pltpu.make_async_copy(book_hbm, own_book, in_sem.at[1])
    fetch_tokens = pltpu.make_async_copy(tokens_hbm, tokens_ref, in_sem.at[2])
    fetch_codes.start()

    def remote(src, dst, ssem, rsem, to):
        return pltpu.make_async_remote_copy(
            src_ref=src,
            dst_ref=dst,
            send_sem=ssem,
            recv_sem=rsem,
            device_id=to,
            device_id_type=pl.DeviceIdType.MESH,
        )

    def copy(send, recv, ssem, rsem, k):
        return remote(send.at[peer[k]], recv.at[me], ssem.at[k], rsem.at[k], at[k])

    def loss_copy(k, other):
        s = other * chips + k
        to = mirror[k] if other else at[k]
        return remote(lsend.at[peer[k]], lrecv.at[other, me], lsem_s.at[s], lsem_r.at[s], to)

    asks = [copy(csend, crecv, csem_s, csem_r, k) for k in order_of if k]
    replies = {k: copy(psend, precv, psem_s, psem_r, k) for k in order_of if k}
    losses = [loss_copy(k, other) for k in order_of for other in (0, 1) if k or other]
    share_book = remote(own_book, own_book, bsem.at[0], bsem.at[1], mirror[0])
    share_asks = remote(dsend, drecv, dsem.at[0], dsem.at[1], mirror[0])

    barrier = pltpu.get_barrier_semaphore()
    for k in order_of:
        for to in (at[k], mirror[k]) if k else (mirror[k],):
            pl.semaphore_signal(
                barrier, inc=1, device_id=to, device_id_type=pl.DeviceIdType.MESH
            )
    fetch_book.start()
    fetch_tokens.start()

    fetch_codes.wait()
    code_row = codes_ref[...].reshape(1, rows)
    hi_row = lax.shift_right_logical(code_row, bits)
    code_col = jnp.broadcast_to(code_row.astype(F32), (128, rows)).T.astype(jnp.int32)
    hi_col = lax.shift_right_logical(code_col, bits)
    lo_col = code_col & (per - 1)
    lane = lax.broadcasted_iota(jnp.int32, (rows, 128), 1)
    own_row = hi_row == lax.broadcasted_iota(jnp.int32, (n, rows), 0)
    for k in range(per // 128):
        low1h[:, k * 128 : (k + 1) * 128] = jnp.where(lo_col == lane + k * 128, 1.0, 0.0).astype(BF16)
    low = low1h[...]
    hist = jnp.dot(jnp.where(own_row, 1.0, 0.0).astype(BF16), low, preferred_element_type=F32)
    odd = (lax.broadcasted_iota(jnp.int32, (n, 128), 0) & 1) == 1

    def first_half(found):
        total = jnp.broadcast_to(jnp.sum(found, axis=1, keepdims=True), (n, 128))
        return total, jnp.where(odd, pltpu.roll(total, 1, 0), 0.0)

    wanted = jnp.where(hist > 0.5, 1.0, 0.0)
    total, ahead = first_half(wanted)
    most = jnp.max(total + ahead, axis=0, keepdims=True)
    heavy = jnp.max(jnp.max(hist, axis=0, keepdims=True), axis=1, keepdims=True) > 256.0
    most = jnp.where(heavy, 256.0, jnp.minimum(most, 256.0))
    most_pair = jnp.broadcast_to(most, (2, EXTRA)).astype(BF16)
    hist16 = hist.astype(BF16)
    for q in range(chips):
        csend[q, :, :per] = hist16[2 * q : 2 * q + 2, :]
        csend[q, :, per:] = most_pair
    crecv[pl.ds(me, 1)] = csend[pl.ds(me, 1)]

    pl.semaphore_wait(barrier, n - 1)
    for ask in asks:
        ask.start()
    fetch_book.wait()
    share_book.start()

    before = lax.broadcasted_iota(jnp.int32, (per, per), 0) < lax.broadcasted_iota(jnp.int32, (per, per), 1)
    before = jnp.where(before, 1.0, 0.0).astype(BF16)
    rank = jnp.dot(wanted.astype(BF16), before, preferred_element_type=F32) + ahead[:, :1]
    rank = jnp.minimum(rank, 255.0).astype(BF16)
    hi1h = jnp.where(hi_col[:, :n] == lane[:, :n], 1.0, 0.0).astype(BF16)
    looked = jnp.dot(hi1h, rank, preferred_element_type=F32).astype(BF16) * low
    found = jnp.dot(looked, jnp.ones((per, 128), BF16), preferred_element_type=F32)
    found = found.astype(jnp.int32)
    rank1h[...] = jnp.where(found == lane, 1.0, 0.0).astype(BF16)
    slot = lax.shift_right_logical(hi_col, 1) * cap + found
    for k in range(chips * cap // 128):
        sel[:, k * 128 : (k + 1) * 128] = jnp.where(slot == lane + k * 128, 1.0, 0.0).astype(BF16)

    for ask in asks:
        ask.wait_recv()
    got = jnp.concatenate([crecv[q].astype(F32) for q in range(chips)], axis=0)
    asked = got[:, :per]
    present = asked > 0.5
    present_one = jnp.where(present, 1.0, 0.0)
    order = jnp.dot(present_one.astype(BF16), before, preferred_element_type=F32)
    order = jnp.where(present, order + first_half(present_one)[1][:, :1], -1.0)
    for q in range(chips):
        ranks[q] = order[2 * q : 2 * q + 2, :]

    share_book.wait_recv()
    place = lax.broadcasted_iota(jnp.int32, (cap, per), 0).astype(F32)
    book = book_ref[...]
    ready = []
    for g in range(0, chips, GROUP):
        group = order_of[g : g + GROUP]
        picks = []
        for k in group:
            pair = ranks[peer[k]]
            picks.append(jnp.concatenate(
                [
                    jnp.where(jnp.broadcast_to(pair[h : h + 1], (cap, per)) == place, 1.0, 0.0).astype(BF16)
                    for h in (0, 1)
                ],
                axis=1,
            ))
        packed = jnp.dot(jnp.concatenate(picks, axis=0), book, preferred_element_type=F32)
        packed = packed.astype(BF16)
        for i, k in enumerate(group):
            out = psend if k else precv
            out[peer[k]] = packed[i * cap : (i + 1) * cap]
        for k in ready:
            replies[k].start()
        ready = [k for k in group if k]
    for k in ready:
        replies[k].start()

    turn = lax.broadcasted_iota(jnp.int32, (n, n), 0)
    side = jnp.where(turn < chips, core, 1 - core)
    which = 2 * lax.rem(turn, chips) + side
    split = jnp.where(lax.broadcasted_iota(jnp.int32, (n, n), 1) == which, 1.0, 0.0).astype(BF16)
    both = jnp.concatenate([order.astype(BF16), jnp.minimum(asked, 256.0).astype(BF16)], axis=1)
    both = jnp.dot(split, both, preferred_element_type=F32)
    most_asked = jnp.max(got[:, per:], axis=0, keepdims=True)
    dsend[:, : 2 * per] = both[chips:]
    dsend[:, 2 * per :] = jnp.broadcast_to(most_asked, (chips, EXTRA))
    share_asks.start()
    share_asks.wait_recv()
    counts = jnp.sum(both[:chips, per:] + drecv[:, per : 2 * per], axis=0, keepdims=True)
    counts_ref[...] = counts.astype(jnp.int32)
    probs = counts / total_tokens
    terms = jnp.where(
        counts > 0.5, probs * jnp.log(jnp.maximum(probs, 1.0 / total_tokens)), 0.0
    )
    entropy = jnp.sum(terms, axis=1, keepdims=True)
    flag_ref[0, 0] = jnp.max(jnp.maximum(most_asked, drecv[:1, 2 * per :])).astype(jnp.int32)
    spots_of = [both[:chips, :per].astype(jnp.int32), drecv[:, :per].astype(jnp.int32)]

    for k in replies:
        replies[k].wait_recv()
    fetch_tokens.wait()
    packs = precv[...].reshape(chips * cap, width)
    quant = jnp.dot(sel[...], packs, preferred_element_type=F32).astype(BF16)
    quant_ref[...] = quant
    diff = tokens_ref[...].astype(F32) - quant.astype(F32)
    square = diff * diff
    folded = square[:, :128]
    for k in range(1, width // 128):
        folded = folded + square[:, k * 128 : (k + 1) * 128]
    tloss = jnp.sum(folded.T, axis=0, keepdims=True) / width
    tloss_ref[...] = tloss
    part = jnp.sum(tloss, axis=1, keepdims=True)

    first = tloss.astype(BF16).astype(F32)
    second = (tloss - first).astype(BF16).astype(F32)
    third = tloss - first - second
    own_chip = lax.shift_right_logical(hi_row, 1) == lax.broadcasted_iota(jnp.int32, (chips, rows), 0)
    spread = jnp.concatenate(
        [jnp.where(own_chip, x, 0.0).astype(BF16) for x in (first, second, third)], axis=0
    )
    sums = jnp.dot(spread, rank1h[...], preferred_element_type=F32)
    sums = sums[:chips] + sums[chips : 2 * chips] + sums[2 * chips :]
    lane1 = lax.broadcasted_iota(jnp.int32, (chips, EXTRA), 1)
    sums = jnp.where(lane1 == EXTRA - 2, part, jnp.where(lane1 == EXTRA - 1, entropy, sums))
    for q in range(chips):
        lsend[q] = sums[q : q + 1, :]
    lrecv[0, pl.ds(me, 1)] = lsend[pl.ds(me, 1)]
    for loss in losses:
        loss.start()

    for ask in asks:
        ask.wait_send()
    for k in replies:
        replies[k].wait_send()
    share_book.wait_send()
    share_asks.wait_send()
    for loss in losses:
        loss.wait_recv()
    added = jnp.zeros((chips, per), F32)
    ends = jnp.zeros((1, EXTRA), F32)
    for other in (0, 1):
        back = lrecv[other, :, 0, :]
        spot = spots_of[other]
        parts = [
            jnp.take_along_axis(back, jnp.maximum(spot[:, j : j + 128], 0), axis=1)
            for j in range(0, per, 128)
        ]
        added = added + jnp.where(spot >= 0, jnp.concatenate(parts, axis=1), 0.0)
        ends = ends + jnp.sum(back, axis=0, keepdims=True)
    closs_ref[...] = jnp.sum(added, axis=0, keepdims=True)
    lane1 = lane1[:1]
    perp = jnp.exp(-ends[:, EXTRA - 1 :])
    scal_ref[...] = jnp.where(lane1 == 0, ends[:, EXTRA - 2 : EXTRA - 1] * (0.25 / total_tokens), perp)
    for loss in losses:
        loss.wait_send()


def send_order(n, cols):
    turns = sorted(range(n // cols), key=lambda d: (abs(2 * d - n // cols), d))
    turns = [d for d in turns if d] + [0]
    blocks = [(d, h) for d in turns for h in (0, 1)]
    half = cols // 2
    spread = sorted(blocks[2:-2], key=lambda b: b[1])
    blocks = blocks[:2] + spread + [(0, 1), (0, 0)]
    return [d * cols + h * half + c for d, h in blocks for c in range(half)]


def exchange(n, cols, cap, number, tokens, codebook, codes):
    rows, width = tokens.shape
    per = codebook.shape[0]
    chips = n // 2
    vmem = pl.BlockSpec(memory_space=pltpu.VMEM)
    smem = pl.BlockSpec(memory_space=pltpu.SMEM)
    dma = pltpu.SemaphoreType.DMA
    return pl.pallas_call(
        functools.partial(kernel, n, cols, cap, send_order(chips, cols // 2)),
        out_shape=(
            jax.ShapeDtypeStruct((rows, width), BF16),
            jax.ShapeDtypeStruct((1, rows), F32),
            jax.ShapeDtypeStruct((1, per), jnp.int32),
            jax.ShapeDtypeStruct((1, per), F32),
            jax.ShapeDtypeStruct((1, EXTRA), F32),
            jax.ShapeDtypeStruct((1, 1), jnp.int32),
        ),
        in_specs=[pl.BlockSpec(memory_space=pltpu.HBM)] * 3,
        out_specs=(vmem, vmem, vmem, vmem, vmem, smem),
        scratch_shapes=[
            pltpu.VMEM(codes.shape, jnp.int32),
            pltpu.VMEM((rows, width), BF16),
            pltpu.VMEM((2 * per, width), BF16),
            pltpu.VMEM((chips, 2, per + EXTRA), BF16),
            pltpu.VMEM((chips, 2, per + EXTRA), BF16),
            pltpu.VMEM((chips, cap, width), BF16),
            pltpu.VMEM((chips, cap, width), BF16),
            pltpu.VMEM((chips, 2 * per + EXTRA), F32),
            pltpu.VMEM((chips, 2 * per + EXTRA), F32),
            pltpu.VMEM((chips, 1, EXTRA), F32),
            pltpu.VMEM((2, chips, 1, EXTRA), F32),
            pltpu.VMEM((chips, 2, per), F32),
            pltpu.VMEM((rows, per), BF16),
            pltpu.VMEM((rows, chips * cap), BF16),
            pltpu.VMEM((rows, 128), BF16),
            dma((3,)),
            dma((chips,)), dma((chips,)), dma((chips,)), dma((chips,)),
            dma((n,)), dma((n,)), dma((2,)), dma((2,)),
        ],
        compiler_params=pltpu.CompilerParams(collective_id=number, has_side_effects=True),
    )(*[pltpu.with_memory_space_constraint(x, pltpu.HBM) for x in (codes, tokens, codebook)])


def finish_kernel(
    quant_ref, tloss_ref, counts_ref, closs_ref, scal_ref,
    quant_out, tloss_out, counts_out, closs_out, commit_out, perp_out, sem,
):
    put = pltpu.make_async_copy(quant_ref, quant_out, sem)
    put.start()
    tloss_out[...] = tloss_ref[...].reshape(tloss_out.shape)
    counts_out[...] = counts_ref[...].reshape(counts_out.shape)
    closs_out[...] = closs_ref[...].reshape(closs_out.shape)
    commit_out[...] = scal_ref[:, :1]
    perp_out[...] = scal_ref[:, 1:2]
    put.wait()


def finish(quantized, token_loss, counts, code_loss, scalars):
    rows, per = token_loss.shape[1], counts.shape[1]
    vmem = pl.BlockSpec(memory_space=pltpu.VMEM)
    q, t, k, c, m, p = pl.pallas_call(
        finish_kernel,
        out_shape=(
            jax.ShapeDtypeStruct(quantized.shape, BF16),
            jax.ShapeDtypeStruct((rows,), F32),
            jax.ShapeDtypeStruct((per,), jnp.int32),
            jax.ShapeDtypeStruct((per,), F32),
            jax.ShapeDtypeStruct((1, 1), F32),
            jax.ShapeDtypeStruct((1, 1), F32),
        ),
        in_specs=[vmem] * 5,
        out_specs=(pl.BlockSpec(memory_space=pltpu.HBM), vmem, vmem, vmem, vmem, vmem),
        scratch_shapes=[pltpu.SemaphoreType.DMA],
    )(quantized, token_loss, counts, code_loss, scalars)
    return q, t, k, c, m[0, 0], p[0, 0]


def asked_plan(n, cols, cap, tokens, codebook, codes):
    *outs, flag = exchange(n, cols, cap, 0, tokens, codebook, codes)

    def kept():
        return finish(*outs)

    def wider():
        return finish(*exchange(n, cols, 2 * cap, 1, tokens, codebook, codes)[:-1])

    def ringed():
        return ring_plan(n, tokens, codebook, codes)

    def any_codes():
        return lax.cond(flag[0, 0] > 2 * cap, ringed, wider)

    return lax.cond(flag[0, 0] > cap, any_codes, kept)


def on_device(n, cols, tokens, codebook, codes):
    rows, width = tokens.shape
    per = codebook.shape[0]
    cap = -(-2 * rows // (n * 16)) * 16
    fits = (
        per % 128 == 0
        and per & (per - 1) == 0
        and rows % 128 == 0
        and width % 128 == 0
        and n // 2 * cap % 128 == 0
        and cols % 8 == 0
        and n // cols > 1
        and n <= 128
        and 2 * cap < EXTRA - 1
    )
    if fits:
        return asked_plan(n, cols, cap, tokens, codebook, codes)
    return dense_plan(tokens, codebook, codes)


def solution(mesh):
    n = mesh.shape["row"] * mesh.shape["col"]
    return jax.shard_map(
        functools.partial(on_device, n, mesh.shape["col"]),
        mesh=mesh,
        in_specs=(P(AXES, None), P(AXES, None), P(AXES)),
        out_specs=(P(AXES, None), P(AXES), P(AXES), P(AXES), P(), P()),
        check_vma=False,
    )
```

time: 37.7 us -> 31.6 us (0.84)
  Pallas kernels: 35.7 us -> 29.6 us
    pallas_call x1, Pallas kernels: 33.2 us -> 28.3 us  [exchange(): pl.pallas_call(functools.partial(kernel, n, cols, cap, send_order(chips,...]
    pallas_call x1, Pallas kernels: 2.57 us -> 1.35 us  [finish(): pl.pallas_call(finish_kernel, out_shape=(jax.ShapeDtypeStruct(quantized.s...]
where the time goes in v2:
time: 31.6 us; the launch traced here: 31.4 us
  Pallas kernels  29.6 us (94%)
  between operations  1.55 us (5%)
    pallas_call x1, Pallas kernels, exchange(): pl.pallas_call(functools.partial(kernel, n, cols, cap, send_order(chips,...  28.3 us
    pallas_call x1, Pallas kernels, finish(): pl.pallas_call(finish_kernel, out_shape=(jax.ShapeDtypeStruct(quantized.s...  1.35 us

profile of v2, /device:TPU:0, one launch (start us, length us, event | category | flops | bytes accessed | tf_op | source)
XLA Modules:
  0.0 31.4 jit_solution(354641093309538665)
XLA Ops:
  0.6 0.0 copy-start
  0.6 0.0 copy-start.2
  0.7 28.3 %shard_map.86 = (bf16[768,256]{1,0:T(8,128)(2,1)S(1)}, f32[1,768]{1,0:T(1,128)S(1)}, s32[1,512]{1,0:T(1,128)S(1)}, f32[1,512]{1,0:T(1,128)S(1)}, f32[1,128]{1,0:T(1,128)S(1)}, /*index=5*/s32[1,1]{1,0:T(1,128)}) custom-call(s32[768]{0:T(1024)} %codes_hbm.1, bf16[768,256]{1,0:T(8,128)(2,1)} %tokens_hbm.1, bf16[512,256]{1,0:T(8,128)(2,1)} %book_hbm.1), custom_call_target="tpu_custom_call" | custom-call | tf_op jit(solution)/shard_map/pallas_call | solution.py:353
  28.9 0.0 copy-start.4
  29.6 0.0 copy-done
  29.6 0.0 copy-done.2
  29.7 0.0 copy-done.4
  29.7 1.6 %conditional.2 = ((bf16[768,256]{1,0:T(8,128)(2,1)}, f32[768]{0:T(1024)}, s32[512]{0:T(512)}, f32[512]{0:T(512)}, f32[]{:T(128)}, /*index=5*/f32[]{:T(128)})) conditional(s32[]{:T(128)} %bitcast.7, (bf16[768,256]{1,0:T(8,128)(2,1)S(1)}, f32[1,768]{1,0:T(1,128)S(1)}, s32[1,512]{1,0:T(1,128)S(1)}, f32[1,512]{1,0:T(1,128)S(1)}, ...), branch_computations={%region_0.0_spmd, %region_1.17_spmd} | conditional | flops 1761645 | bytes 4995427 | solution.py:438
  29.7 1.4 %branch_0_fun.3 = (bf16[768,256]{1,0:T(8,128)(2,1)}, f32[768]{0:T(1024)}, s32[512]{0:T(512)}, f32[512]{0:T(512)}, f32[1,1]{1,0:T(1,128)}, /*index=5*/f32[1,1]{1,0:T(1,128)}) custom-call(bf16[768,256]{1,0:T(8,128)(2,1)S(1)} %get-tuple-element.374.quant_ref, f32[1,768]{1,0:T(1,128)S(1)} %get-tuple-element.375.tloss_ref, ...), custom_call_target="tpu_custom_call" | custom-call | tf_op jit(solution)/shard_map/cond/branch_0_fun/pallas_call | solution.py:406
Async XLA Ops:
  0.6 29.0 %copy-start = (bf16[768,256]{1,0:T(8,128)(2,1)S(1)}, bf16[768,256]{1,0:T(8,128)(2,1)}, u32[]{:S(2)}) copy-start(bf16[768,256]{1,0:T(8,128)(2,1)} %tokens_hbm.1) | copy-start | bytes 1179652
  0.6 29.0 %copy-start.2 = (bf16[512,256]{1,0:T(8,128)(2,1)S(1)}, bf16[512,256]{1,0:T(8,128)(2,1)}, u32[]{:S(2)}) copy-start(bf16[512,256]{1,0:T(8,128)(2,1)} %book_hbm.1) | copy-start | bytes 786436
  28.9 0.7 %copy-start.4 = (s32[768]{0:T(1024)S(1)}, s32[768]{0:T(1024)}, u32[]{:S(2)}) copy-start(s32[768]{0:T(1024)} %codes_hbm.1) | copy-start | bytes 9220

commit v3 on v2

--- a/solution.py
+++ b/solution.py
@@ -9,7 +9,8 @@
 
 AXES = ("row", "col")
 EXTRA = 128
-GROUP = 4
+ASK_ORDER = (3, 2, 1, 0)
+REPLY_ORDER = (2, 3, 1, 0)
 F32 = jnp.float32
 BF16 = jnp.bfloat16
 
@@ -105,12 +106,13 @@
 
 
 def kernel(
-    n, cols, cap, order_of,
+    n, cols, cap, spill, wide_spill,
     codes_hbm, tokens_hbm, book_hbm,
     quant_ref, tloss_ref, counts_ref, closs_ref, scal_ref, flag_ref,
-    codes_ref, tokens_ref, book_ref, csend, crecv, psend, precv, dsend, drecv, lsend, lrecv,
-    ranks, low1h, sel, rank1h,
-    in_sem, csem_s, csem_r, psem_s, psem_r, lsem_s, lsem_r, bsem, dsem,
+    codes_ref, tokens_ref, book_ref, csend, crecv, hsend, hrecv, psend, precv, gsend, grecv, osend, orecv,
+    dsend, drecv, lsend, lrecv, low1h, sel, spill1h, rank1h,
+    in_sem, csem_s, csem_r, hsem_s, hsem_r, psem_s, psem_r,
+    gsem_s, gsem_r, osem_s, osem_r, lsem_s, lsem_r, bsem, dsem,
 ):
     rows, width = tokens_hbm.shape
     per = book_hbm.shape[0]
@@ -121,8 +123,14 @@
     core = lax.rem(my_col, 2)
     my_chip = lax.div(my_col, 2)
     me = my_row * half + my_chip
-    rows_at = [lax.rem(my_row + d, chips // half) for d in range(chips // half)]
-    chips_at = [lax.rem(my_chip + d, half) for d in range(half)]
+    inner = lax.rem(lax.div(my_row + 1, 2), 2)
+    beside, across = my_row + 1 - 2 * lax.rem(my_row, 2), 3 - my_row
+    near = inner * across + (1 - inner) * beside
+    far = inner * beside + (1 - inner) * across
+    rows_at = [my_row, near, lax.rem(my_row + 2, 4), far]
+    chips_at = [
+        my_chip, my_chip + 1 - 2 * lax.rem(my_chip, 2), lax.rem(my_chip + 2, 4), 3 - my_chip
+    ]
     spots = [(rows_at[k // half], chips_at[k % half]) for k in range(chips)]
     at = [(r, 2 * c + core) for r, c in spots]
     mirror = [(r, 2 * c + 1 - core) for r, c in spots]
@@ -143,26 +151,43 @@
             device_id_type=pl.DeviceIdType.MESH,
         )
 
-    def copy(send, recv, ssem, rsem, k):
-        return remote(send.at[peer[k]], recv.at[me], ssem.at[k], rsem.at[k], at[k])
-
-    def loss_copy(k, other):
-        s = other * chips + k
+    def put(send, recv, ssem, rsem, k):
+        return remote(send.at[peer[k]], recv.at[me], ssem, rsem, at[k])
+
+    def spill_put(d, c):
+        r, to = rows_at[d], chips_at[c]
+        return remote(gsend.at[r, to], grecv.at[r, my_chip], gsem_s, gsem_r.at[r], at[c])
+
+    def joint_put(d):
+        return remote(osend.at[rows_at[d]], orecv.at[my_row], osem_s, osem_r, at[d * half])
+
+    def loss_put(k, other):
         to = mirror[k] if other else at[k]
-        return remote(lsend.at[peer[k]], lrecv.at[other, me], lsem_s.at[s], lsem_r.at[s], to)
-
-    asks = [copy(csend, crecv, csem_s, csem_r, k) for k in order_of if k]
-    replies = {k: copy(psend, precv, psem_s, psem_r, k) for k in order_of if k}
-    losses = [loss_copy(k, other) for k in order_of for other in (0, 1) if k or other]
+        return remote(lsend.at[peer[k]], lrecv.at[other * chips + me], lsem_s, lsem_r, to)
+
+    def all_in(ref, count, sem):
+        part = ref.at[pl.ds(0, count)]
+        remote(part, part, sem, sem, mirror[0]).wait_recv()
+
+    def all_out(ref, count, sem):
+        part = ref.at[pl.ds(0, count)]
+        remote(part, part, sem, sem, mirror[0]).wait_send()
+
+    ask_refs = (csend, crecv, csem_s, csem_r.at[my_row])
+    count_refs = (hsend, hrecv, hsem_s, hsem_r)
+    reply_refs = (psend, precv, psem_s, psem_r)
+    partners = [k for d in ASK_ORDER for k in range(d * half, d * half + half) if k]
+    everyone = [(k, other) for d in ASK_ORDER for k in range(d * half, d * half + half)
+                for other in (0, 1) if k or other]
     share_book = remote(own_book, own_book, bsem.at[0], bsem.at[1], mirror[0])
     share_asks = remote(dsend, drecv, dsem.at[0], dsem.at[1], mirror[0])
 
     barrier = pltpu.get_barrier_semaphore()
-    for k in order_of:
-        for to in (at[k], mirror[k]) if k else (mirror[k],):
-            pl.semaphore_signal(
-                barrier, inc=1, device_id=to, device_id_type=pl.DeviceIdType.MESH
-            )
+    for k, other in everyone:
+        pl.semaphore_signal(
+            barrier, inc=1, device_id=mirror[k] if other else at[k],
+            device_id_type=pl.DeviceIdType.MESH,
+        )
     fetch_book.start()
     fetch_tokens.start()
 
@@ -186,78 +211,113 @@
 
     wanted = jnp.where(hist > 0.5, 1.0, 0.0)
     total, ahead = first_half(wanted)
-    most = jnp.max(total + ahead, axis=0, keepdims=True)
+    both = total + ahead
+    over = [jnp.where(odd, jnp.maximum(both - float(c), 0.0), 0.0) for c in (cap, 2 * cap)]
+    over = jnp.minimum(jnp.concatenate(over, axis=1), 256.0).astype(BF16)
+    line = lax.broadcasted_iota(jnp.int32, (2 * n, n), 0)
+    source = lax.broadcasted_iota(jnp.int32, (2 * n, n), 1)
+    line_of = lax.rem(line, n)
+    same = lax.div(line_of, cols) == lax.div(source, cols)
+    earlier = lax.div(source, 2) < lax.div(line_of, 2)
+    reach = jnp.where(same & (earlier | (line >= n)), 1.0, 0.0).astype(BF16)
+    over = jnp.dot(reach, over, preferred_element_type=F32)
+    behind = over[:n, :1]
+    worst = jnp.max(over[n:], axis=0, keepdims=True)
     heavy = jnp.max(jnp.max(hist, axis=0, keepdims=True), axis=1, keepdims=True) > 256.0
-    most = jnp.where(heavy, 256.0, jnp.minimum(most, 256.0))
+    most = jnp.where(worst[:, EXTRA:] > float(wide_spill), 2.0, 1.0)
+    most = jnp.where(worst[:, :EXTRA] > float(spill), most, 0.0)
+    most = jnp.where(heavy, 2.0, most)
     most_pair = jnp.broadcast_to(most, (2, EXTRA)).astype(BF16)
-    hist16 = hist.astype(BF16)
-    for q in range(chips):
-        csend[q, :, :per] = hist16[2 * q : 2 * q + 2, :]
-        csend[q, :, per:] = most_pair
-    crecv[pl.ds(me, 1)] = csend[pl.ds(me, 1)]
-
-    pl.semaphore_wait(barrier, n - 1)
-    for ask in asks:
-        ask.start()
-    fetch_book.wait()
-    share_book.start()
-
     before = lax.broadcasted_iota(jnp.int32, (per, per), 0) < lax.broadcasted_iota(jnp.int32, (per, per), 1)
     before = jnp.where(before, 1.0, 0.0).astype(BF16)
     rank = jnp.dot(wanted.astype(BF16), before, preferred_element_type=F32) + ahead[:, :1]
-    rank = jnp.minimum(rank, 255.0).astype(BF16)
+    rank = jnp.minimum(rank + jnp.where(rank > cap - 0.5, behind, 0.0), 255.0)
+    order = jnp.where(wanted > 0.5, rank, -1.0).astype(BF16)
+    for q in range(chips):
+        csend[q, :, :per] = order[2 * q : 2 * q + 2, :]
+        csend[q, :, per:] = most_pair
+    crecv[pl.ds(me, 1)] = csend[pl.ds(me, 1)]
+
+    pl.semaphore_wait(barrier, n - 1)
+    for k in partners:
+        put(*ask_refs, k).start()
+    hist16 = jnp.minimum(hist, 256.0).astype(BF16)
+    for q in range(chips):
+        hsend[q] = hist16[2 * q : 2 * q + 2, :]
+    hrecv[pl.ds(me, 1)] = hsend[pl.ds(me, 1)]
+    fetch_book.wait()
+    share_book.start()
+    for k in partners:
+        put(*count_refs, k).start()
+
+    rank = rank.astype(BF16)
     hi1h = jnp.where(hi_col[:, :n] == lane[:, :n], 1.0, 0.0).astype(BF16)
     looked = jnp.dot(hi1h, rank, preferred_element_type=F32).astype(BF16) * low
     found = jnp.dot(looked, jnp.ones((per, 128), BF16), preferred_element_type=F32)
     found = found.astype(jnp.int32)
     rank1h[...] = jnp.where(found == lane, 1.0, 0.0).astype(BF16)
-    slot = lax.shift_right_logical(hi_col, 1) * cap + found
+    chip_col = lax.shift_right_logical(hi_col, 1)
+    slot = jnp.where(found < cap, chip_col * cap + found, -1)
     for k in range(chips * cap // 128):
         sel[:, k * 128 : (k + 1) * 128] = jnp.where(slot == lane + k * 128, 1.0, 0.0).astype(BF16)
-
-    for ask in asks:
-        ask.wait_recv()
-    got = jnp.concatenate([crecv[q].astype(F32) for q in range(chips)], axis=0)
-    asked = got[:, :per]
-    present = asked > 0.5
-    present_one = jnp.where(present, 1.0, 0.0)
-    order = jnp.dot(present_one.astype(BF16), before, preferred_element_type=F32)
-    order = jnp.where(present, order + first_half(present_one)[1][:, :1], -1.0)
-    for q in range(chips):
-        ranks[q] = order[2 * q : 2 * q + 2, :]
-
-    share_book.wait_recv()
-    place = lax.broadcasted_iota(jnp.int32, (cap, per), 0).astype(F32)
-    book = book_ref[...]
-    ready = []
-    for g in range(0, chips, GROUP):
-        group = order_of[g : g + GROUP]
+    slot = jnp.where(found < cap, -1, lax.div(chip_col, half) * spill + (found - cap))
+    planes = chips // half
+    for k in range(0, planes * spill, 128):
+        wide = min(128, planes * spill - k)
+        spill1h[:, k : k + wide] = jnp.where(slot == lane + k, 1.0, 0.0).astype(BF16)[:, :wide]
+
+    both_caps = cap + spill
+    place = lax.broadcasted_iota(jnp.int32, (both_caps, per), 0).astype(F32)
+    for i, d in enumerate(REPLY_ORDER):
+        group = range(d * half, d * half + half)
+        all_in(crecv, half if d else half - 1, csem_r.at[rows_at[d]])
+        if i == 0:
+            share_book.wait_recv()
         picks = []
         for k in group:
-            pair = ranks[peer[k]]
+            pair = crecv[peer[k]][:, :per].astype(F32)
             picks.append(jnp.concatenate(
                 [
-                    jnp.where(jnp.broadcast_to(pair[h : h + 1], (cap, per)) == place, 1.0, 0.0).astype(BF16)
+                    jnp.where(jnp.broadcast_to(pair[h : h + 1], (both_caps, per)) == place, 1.0, 0.0).astype(BF16)
                     for h in (0, 1)
                 ],
                 axis=1,
             ))
-        packed = jnp.dot(jnp.concatenate(picks, axis=0), book, preferred_element_type=F32)
+        packed = jnp.dot(jnp.concatenate(picks, axis=0), book_ref[...], preferred_element_type=F32)
         packed = packed.astype(BF16)
-        for i, k in enumerate(group):
+        for j, k in enumerate(group):
             out = psend if k else precv
-            out[peer[k]] = packed[i * cap : (i + 1) * cap]
-        for k in ready:
-            replies[k].start()
-        ready = [k for k in group if k]
-    for k in ready:
-        replies[k].start()
-
+            start = j * both_caps
+            out[peer[k]] = packed[start : start + cap]
+            if j:
+                gsend[rows_at[d], chips_at[j]] = packed[start + cap : start + both_caps]
+            else:
+                grecv[rows_at[d], my_chip] = packed[start + cap : start + both_caps]
+        for c in range(1, half):
+            spill_put(d, c).start()
+        for k in group:
+            if k:
+                put(*reply_refs, k).start()
+
+    for d in REPLY_ORDER:
+        all_in(grecv.at[0], half - 1, gsem_r.at[rows_at[d]])
+        joint = grecv[rows_at[d], 0].astype(F32)
+        for c in range(1, half):
+            joint = joint + grecv[rows_at[d], c].astype(F32)
+        if d:
+            osend[rows_at[d]] = joint.astype(BF16)
+            joint_put(d).start()
+        else:
+            orecv[my_row] = joint.astype(BF16)
+
+    all_in(hrecv, chips - 1, hsem_r)
+    got = jnp.concatenate([crecv[q].astype(F32) for q in range(chips)], axis=0)
+    asked = jnp.concatenate([hrecv[q].astype(F32) for q in range(chips)], axis=0)
     turn = lax.broadcasted_iota(jnp.int32, (n, n), 0)
     side = jnp.where(turn < chips, core, 1 - core)
     which = 2 * lax.rem(turn, chips) + side
     split = jnp.where(lax.broadcasted_iota(jnp.int32, (n, n), 1) == which, 1.0, 0.0).astype(BF16)
-    both = jnp.concatenate([order.astype(BF16), jnp.minimum(asked, 256.0).astype(BF16)], axis=1)
+    both = jnp.concatenate([got[:, :per].astype(BF16), asked.astype(BF16)], axis=1)
     both = jnp.dot(split, both, preferred_element_type=F32)
     most_asked = jnp.max(got[:, per:], axis=0, keepdims=True)
     dsend[:, : 2 * per] = both[chips:]
@@ -274,11 +334,13 @@
     flag_ref[0, 0] = jnp.max(jnp.maximum(most_asked, drecv[:1, 2 * per :])).astype(jnp.int32)
     spots_of = [both[:chips, :per].astype(jnp.int32), drecv[:, :per].astype(jnp.int32)]
 
-    for k in replies:
-        replies[k].wait_recv()
+    all_in(precv, chips - 1, psem_r)
     fetch_tokens.wait()
     packs = precv[...].reshape(chips * cap, width)
-    quant = jnp.dot(sel[...], packs, preferred_element_type=F32).astype(BF16)
+    direct = jnp.dot(sel[...], packs, preferred_element_type=F32)
+    all_in(orecv, planes - 1, osem_r)
+    packs = orecv[...].reshape(planes * spill, width)
+    quant = (direct + jnp.dot(spill1h[...], packs, preferred_element_type=F32)).astype(BF16)
     quant_ref[...] = quant
     diff = tokens_ref[...].astype(F32) - quant.astype(F32)
     square = diff * diff
@@ -302,22 +364,22 @@
     sums = jnp.where(lane1 == EXTRA - 2, part, jnp.where(lane1 == EXTRA - 1, entropy, sums))
     for q in range(chips):
         lsend[q] = sums[q : q + 1, :]
-    lrecv[0, pl.ds(me, 1)] = lsend[pl.ds(me, 1)]
-    for loss in losses:
-        loss.start()
-
-    for ask in asks:
-        ask.wait_send()
-    for k in replies:
-        replies[k].wait_send()
+    lrecv[pl.ds(me, 1)] = lsend[pl.ds(me, 1)]
+    for k, other in everyone:
+        loss_put(k, other).start()
+
+    all_out(csend, chips - 1, csem_s)
+    all_out(hsend, chips - 1, hsem_s)
+    all_out(psend, chips - 1, psem_s)
+    all_out(gsend, planes - 1, gsem_s)
+    all_out(osend, planes - 1, osem_s)
     share_book.wait_send()
     share_asks.wait_send()
-    for loss in losses:
-        loss.wait_recv()
+    all_in(lrecv, n - 1, lsem_r)
     added = jnp.zeros((chips, per), F32)
     ends = jnp.zeros((1, EXTRA), F32)
     for other in (0, 1):
-        back = lrecv[other, :, 0, :]
+        back = lrecv[other * chips : (other + 1) * chips, 0, :]
         spot = spots_of[other]
         parts = [
             jnp.take_along_axis(back, jnp.maximum(spot[:, j : j + 128], 0), axis=1)
@@ -329,29 +391,18 @@
     lane1 = lane1[:1]
     perp = jnp.exp(-ends[:, EXTRA - 1 :])
     scal_ref[...] = jnp.where(lane1 == 0, ends[:, EXTRA - 2 : EXTRA - 1] * (0.25 / total_tokens), perp)
-    for loss in losses:
-        loss.wait_send()
-
-
-def send_order(n, cols):
-    turns = sorted(range(n // cols), key=lambda d: (abs(2 * d - n // cols), d))
-    turns = [d for d in turns if d] + [0]
-    blocks = [(d, h) for d in turns for h in (0, 1)]
-    half = cols // 2
-    spread = sorted(blocks[2:-2], key=lambda b: b[1])
-    blocks = blocks[:2] + spread + [(0, 1), (0, 0)]
-    return [d * cols + h * half + c for d, h in blocks for c in range(half)]
-
-
-def exchange(n, cols, cap, number, tokens, codebook, codes):
+    all_out(lrecv, n - 1, lsem_s)
+
+
+def exchange(n, cols, cap, spill, wide_spill, number, tokens, codebook, codes):
     rows, width = tokens.shape
     per = codebook.shape[0]
-    chips = n // 2
+    chips, planes = n // 2, n // cols
     vmem = pl.BlockSpec(memory_space=pltpu.VMEM)
     smem = pl.BlockSpec(memory_space=pltpu.SMEM)
     dma = pltpu.SemaphoreType.DMA
     return pl.pallas_call(
-        functools.partial(kernel, n, cols, cap, send_order(chips, cols // 2)),
+        functools.partial(kernel, n, cols, cap, spill, wide_spill),
         out_shape=(
             jax.ShapeDtypeStruct((rows, width), BF16),
             jax.ShapeDtypeStruct((1, rows), F32),
@@ -368,19 +419,26 @@
             pltpu.VMEM((2 * per, width), BF16),
             pltpu.VMEM((chips, 2, per + EXTRA), BF16),
             pltpu.VMEM((chips, 2, per + EXTRA), BF16),
+            pltpu.VMEM((chips, 2, per), BF16),
+            pltpu.VMEM((chips, 2, per), BF16),
             pltpu.VMEM((chips, cap, width), BF16),
             pltpu.VMEM((chips, cap, width), BF16),
+            pltpu.VMEM((planes, cols // 2, spill, width), BF16),
+            pltpu.VMEM((planes, cols // 2, spill, width), BF16),
+            pltpu.VMEM((planes, spill, width), BF16),
+            pltpu.VMEM((planes, spill, width), BF16),
             pltpu.VMEM((chips, 2 * per + EXTRA), F32),
             pltpu.VMEM((chips, 2 * per + EXTRA), F32),
             pltpu.VMEM((chips, 1, EXTRA), F32),
-            pltpu.VMEM((2, chips, 1, EXTRA), F32),
-            pltpu.VMEM((chips, 2, per), F32),
+            pltpu.VMEM((n, 1, EXTRA), F32),
             pltpu.VMEM((rows, per), BF16),
             pltpu.VMEM((rows, chips * cap), BF16),
+            pltpu.VMEM((rows, planes * spill), BF16),
             pltpu.VMEM((rows, 128), BF16),
             dma((3,)),
-            dma((chips,)), dma((chips,)), dma((chips,)), dma((chips,)),
-            dma((n,)), dma((n,)), dma((2,)), dma((2,)),
+            dma, dma((planes,)), *[dma] * 4,
+            dma, dma((planes,)), *[dma] * 4,
+            dma((2,)), dma((2,)),
         ],
         compiler_params=pltpu.CompilerParams(collective_id=number, has_side_effects=True),
     )(*[pltpu.with_memory_space_constraint(x, pltpu.HBM) for x in (codes, tokens, codebook)])
@@ -420,41 +478,45 @@
     return q, t, k, c, m[0, 0], p[0, 0]
 
 
-def asked_plan(n, cols, cap, tokens, codebook, codes):
-    *outs, flag = exchange(n, cols, cap, 0, tokens, codebook, codes)
+def asked_plan(n, cols, cap, spill, tokens, codebook, codes):
+    wide = spill * 3 // 2
+    *outs, flag = exchange(n, cols, cap, spill, wide, 0, tokens, codebook, codes)
 
     def kept():
         return finish(*outs)
 
     def wider():
-        return finish(*exchange(n, cols, 2 * cap, 1, tokens, codebook, codes)[:-1])
+        return finish(*exchange(n, cols, 2 * cap, wide, wide, 1, tokens, codebook, codes)[:-1])
 
     def ringed():
         return ring_plan(n, tokens, codebook, codes)
 
     def any_codes():
-        return lax.cond(flag[0, 0] > 2 * cap, ringed, wider)
-
-    return lax.cond(flag[0, 0] > cap, any_codes, kept)
+        return lax.cond(flag[0, 0] > 1, ringed, wider)
+
+    return lax.cond(flag[0, 0] > 0, any_codes, kept)
 
 
 def on_device(n, cols, tokens, codebook, codes):
     rows, width = tokens.shape
     per = codebook.shape[0]
-    cap = -(-2 * rows // (n * 16)) * 16
+    cap = -(-rows // (n * 16)) * 16
+    spill = cap
     fits = (
         per % 128 == 0
         and per & (per - 1) == 0
         and rows % 128 == 0
         and width % 128 == 0
         and n // 2 * cap % 128 == 0
-        and cols % 8 == 0
-        and n // cols > 1
+        and n // cols * spill % 128 == 0
+        and n // cols * (spill * 3 // 2) % 64 == 0
+        and cols == 8
+        and n == 4 * cols
         and n <= 128
-        and 2 * cap < EXTRA - 1
+        and 2 * cap + spill * 3 // 2 < EXTRA - 1
     )
     if fits:
-        return asked_plan(n, cols, cap, tokens, codebook, codes)
+        return asked_plan(n, cols, cap, spill, tokens, codebook, codes)
     return dense_plan(tokens, codebook, codes)
 
 

time: 31.6 us -> 29 us (0.918)
  Pallas kernels: 29.6 us -> 27 us
    pallas_call x1, Pallas kernels: 28.3 us -> 25.6 us  [exchange(): pl.pallas_call(functools.partial(kernel, n, cols, cap, spill, wide_spill)...]
where the time goes in v3:
time: 29 us; the launch traced here: 28.8 us
  Pallas kernels  27 us (93%)
  between operations  1.55 us (5%)
    pallas_call x1, Pallas kernels, exchange(): pl.pallas_call(functools.partial(kernel, n, cols, cap, spill, wide_spill)...  25.6 us
    pallas_call x1, Pallas kernels, finish(): pl.pallas_call(finish_kernel, out_shape=(jax.ShapeDtypeStruct(quantized.s...  1.35 us

profile of v3, /device:TPU:0, one launch (start us, length us, event | category | flops | bytes accessed | tf_op | source)
XLA Modules:
  0.0 28.8 jit_solution(291087131784025313)
XLA Ops:
  0.6 0.0 copy-start
  0.6 0.0 copy-start.2
  0.7 25.6 %shard_map.86 = (bf16[768,256]{1,0:T(8,128)(2,1)S(1)}, f32[1,768]{1,0:T(1,128)S(1)}, s32[1,512]{1,0:T(1,128)S(1)}, f32[1,512]{1,0:T(1,128)S(1)}, f32[1,128]{1,0:T(1,128)S(1)}, /*index=5*/s32[1,1]{1,0:T(1,128)}) custom-call(s32[768]{0:T(1024)} %codes_hbm.1, bf16[768,256]{1,0:T(8,128)(2,1)} %tokens_hbm.1, bf16[512,256]{1,0:T(8,128)(2,1)} %book_hbm.1), custom_call_target="tpu_custom_call" | custom-call | tf_op jit(solution)/shard_map/pallas_call | solution.py:404
  26.3 0.0 copy-start.4
  27.0 0.0 copy-done
  27.0 0.0 copy-done.2
  27.0 0.0 copy-done.4
  27.0 1.6 %conditional.2 = ((bf16[768,256]{1,0:T(8,128)(2,1)}, f32[768]{0:T(1024)}, s32[512]{0:T(512)}, f32[512]{0:T(512)}, f32[]{:T(128)}, /*index=5*/f32[]{:T(128)})) conditional(s32[]{:T(128)} %bitcast.7, (bf16[768,256]{1,0:T(8,128)(2,1)S(1)}, f32[1,768]{1,0:T(1,128)S(1)}, s32[1,512]{1,0:T(1,128)S(1)}, f32[1,512]{1,0:T(1,128)S(1)}, ...), branch_computations={%region_0.0_spmd, %region_1.17_spmd} | conditional | flops 1761645 | bytes 4995427 | solution.py:497
  27.0 1.4 %branch_0_fun.3 = (bf16[768,256]{1,0:T(8,128)(2,1)}, f32[768]{0:T(1024)}, s32[512]{0:T(512)}, f32[512]{0:T(512)}, f32[1,1]{1,0:T(1,128)}, /*index=5*/f32[1,1]{1,0:T(1,128)}) custom-call(bf16[768,256]{1,0:T(8,128)(2,1)S(1)} %get-tuple-element.374.quant_ref, f32[1,768]{1,0:T(1,128)S(1)} %get-tuple-element.375.tloss_ref, ...), custom_call_target="tpu_custom_call" | custom-call | tf_op jit(solution)/shard_map/cond/branch_0_fun/pallas_call | solution.py:464
Async XLA Ops:
  0.6 26.4 %copy-start = (bf16[768,256]{1,0:T(8,128)(2,1)S(1)}, bf16[768,256]{1,0:T(8,128)(2,1)}, u32[]{:S(2)}) copy-start(bf16[768,256]{1,0:T(8,128)(2,1)} %tokens_hbm.1) | copy-start | bytes 1179652
  0.6 26.4 %copy-start.2 = (bf16[512,256]{1,0:T(8,128)(2,1)S(1)}, bf16[512,256]{1,0:T(8,128)(2,1)}, u32[]{:S(2)}) copy-start(bf16[512,256]{1,0:T(8,128)(2,1)} %book_hbm.1) | copy-start | bytes 786436
  26.3 0.7 %copy-start.4 = (s32[768]{0:T(1024)S(1)}, s32[768]{0:T(1024)}, u32[]{:S(2)}) copy-start(s32[768]{0:T(1024)} %codes_hbm.1) | copy-start | bytes 9220

commit v4 on v3

--- a/solution.py
+++ b/solution.py
@@ -108,7 +108,7 @@
 def kernel(
     n, cols, cap, spill, wide_spill,
     codes_hbm, tokens_hbm, book_hbm,
-    quant_ref, tloss_ref, counts_ref, closs_ref, scal_ref, flag_ref,
+    quant_ref, tloss_ref, counts_ref, closs_ref, scal_ref,
     codes_ref, tokens_ref, book_ref, csend, crecv, hsend, hrecv, psend, precv, gsend, grecv, osend, orecv,
     dsend, drecv, lsend, lrecv, low1h, sel, spill1h, rank1h,
     in_sem, csem_s, csem_r, hsem_s, hsem_r, psem_s, psem_r,
@@ -266,7 +266,7 @@
         wide = min(128, planes * spill - k)
         spill1h[:, k : k + wide] = jnp.where(slot == lane + k, 1.0, 0.0).astype(BF16)[:, :wide]
 
-    both_caps = cap + spill
+    both_caps = cap + -(-spill // 16) * 16
     place = lax.broadcasted_iota(jnp.int32, (both_caps, per), 0).astype(F32)
     for i, d in enumerate(REPLY_ORDER):
         group = range(d * half, d * half + half)
@@ -290,9 +290,9 @@
             start = j * both_caps
             out[peer[k]] = packed[start : start + cap]
             if j:
-                gsend[rows_at[d], chips_at[j]] = packed[start + cap : start + both_caps]
+                gsend[rows_at[d], chips_at[j]] = packed[start + cap : start + cap + spill]
             else:
-                grecv[rows_at[d], my_chip] = packed[start + cap : start + both_caps]
+                grecv[rows_at[d], my_chip] = packed[start + cap : start + cap + spill]
         for c in range(1, half):
             spill_put(d, c).start()
         for k in group:
@@ -331,7 +331,7 @@
         counts > 0.5, probs * jnp.log(jnp.maximum(probs, 1.0 / total_tokens)), 0.0
     )
     entropy = jnp.sum(terms, axis=1, keepdims=True)
-    flag_ref[0, 0] = jnp.max(jnp.maximum(most_asked, drecv[:1, 2 * per :])).astype(jnp.int32)
+    flag = jnp.maximum(most_asked, drecv[:1, 2 * per :])
     spots_of = [both[:chips, :per].astype(jnp.int32), drecv[:, :per].astype(jnp.int32)]
 
     all_in(precv, chips - 1, psem_r)
@@ -390,7 +390,8 @@
     closs_ref[...] = jnp.sum(added, axis=0, keepdims=True)
     lane1 = lane1[:1]
     perp = jnp.exp(-ends[:, EXTRA - 1 :])
-    scal_ref[...] = jnp.where(lane1 == 0, ends[:, EXTRA - 2 : EXTRA - 1] * (0.25 / total_tokens), perp)
+    commit = ends[:, EXTRA - 2 : EXTRA - 1] * (0.25 / total_tokens)
+    scal_ref[...] = jnp.where(lane1 == 0, commit, jnp.where(lane1 == 1, perp, flag))
     all_out(lrecv, n - 1, lsem_s)
 
 
@@ -399,20 +400,18 @@
     per = codebook.shape[0]
     chips, planes = n // 2, n // cols
     vmem = pl.BlockSpec(memory_space=pltpu.VMEM)
-    smem = pl.BlockSpec(memory_space=pltpu.SMEM)
     dma = pltpu.SemaphoreType.DMA
     return pl.pallas_call(
         functools.partial(kernel, n, cols, cap, spill, wide_spill),
         out_shape=(
-            jax.ShapeDtypeStruct((rows, width), BF16),
-            jax.ShapeDtypeStruct((1, rows), F32),
-            jax.ShapeDtypeStruct((1, per), jnp.int32),
-            jax.ShapeDtypeStruct((1, per), F32),
-            jax.ShapeDtypeStruct((1, EXTRA), F32),
-            jax.ShapeDtypeStruct((1, 1), jnp.int32),
+            pltpu.VMEM((rows, width), BF16),
+            pltpu.VMEM((1, rows), F32),
+            pltpu.VMEM((1, per), jnp.int32),
+            pltpu.VMEM((1, per), F32),
+            pltpu.VMEM((1, EXTRA), F32),
         ),
         in_specs=[pl.BlockSpec(memory_space=pltpu.HBM)] * 3,
-        out_specs=(vmem, vmem, vmem, vmem, vmem, smem),
+        out_specs=(vmem,) * 5,
         scratch_shapes=[
             pltpu.VMEM(codes.shape, jnp.int32),
             pltpu.VMEM((rows, width), BF16),
@@ -446,7 +445,7 @@
 
 def finish_kernel(
     quant_ref, tloss_ref, counts_ref, closs_ref, scal_ref,
-    quant_out, tloss_out, counts_out, closs_out, commit_out, perp_out, sem,
+    quant_out, tloss_out, counts_out, closs_out, commit_out, perp_out, flag_out, sem,
 ):
     put = pltpu.make_async_copy(quant_ref, quant_out, sem)
     put.start()
@@ -455,13 +454,14 @@
     closs_out[...] = closs_ref[...].reshape(closs_out.shape)
     commit_out[...] = scal_ref[:, :1]
     perp_out[...] = scal_ref[:, 1:2]
+    flag_out[...] = scal_ref[:, 2:3].astype(jnp.int32)
     put.wait()
 
 
 def finish(quantized, token_loss, counts, code_loss, scalars):
     rows, per = token_loss.shape[1], counts.shape[1]
     vmem = pl.BlockSpec(memory_space=pltpu.VMEM)
-    q, t, k, c, m, p = pl.pallas_call(
+    q, t, k, c, m, p, f = pl.pallas_call(
         finish_kernel,
         out_shape=(
             jax.ShapeDtypeStruct(quantized.shape, BF16),
@@ -470,23 +470,27 @@
             jax.ShapeDtypeStruct((per,), F32),
             jax.ShapeDtypeStruct((1, 1), F32),
             jax.ShapeDtypeStruct((1, 1), F32),
+            jax.ShapeDtypeStruct((1, 1), jnp.int32),
         ),
         in_specs=[vmem] * 5,
-        out_specs=(pl.BlockSpec(memory_space=pltpu.HBM), vmem, vmem, vmem, vmem, vmem),
+        out_specs=(pl.BlockSpec(memory_space=pltpu.HBM), vmem, vmem, vmem, vmem, vmem, vmem),
         scratch_shapes=[pltpu.SemaphoreType.DMA],
+        compiler_params=pltpu.CompilerParams(vmem_limit_bytes=4 << 20),
     )(quantized, token_loss, counts, code_loss, scalars)
-    return q, t, k, c, m[0, 0], p[0, 0]
+    return q, t, k, c, m[0, 0], p[0, 0], f
 
 
 def asked_plan(n, cols, cap, spill, tokens, codebook, codes):
-    wide = spill * 3 // 2
-    *outs, flag = exchange(n, cols, cap, spill, wide, 0, tokens, codebook, codes)
+    wide = spill * 2
+    outs = exchange(n, cols, cap, spill, wide, 0, tokens, codebook, codes)
+
+    *done, flag = finish(*outs)
 
     def kept():
-        return finish(*outs)
+        return tuple(done)
 
     def wider():
-        return finish(*exchange(n, cols, 2 * cap, wide, wide, 1, tokens, codebook, codes)[:-1])
+        return finish(*exchange(n, cols, 2 * cap, wide, wide, 1, tokens, codebook, codes))[:-1]
 
     def ringed():
         return ring_plan(n, tokens, codebook, codes)
@@ -501,19 +505,18 @@
     rows, width = tokens.shape
     per = codebook.shape[0]
     cap = -(-rows // (n * 16)) * 16
-    spill = cap
+    spill = cap * 3 // 4
     fits = (
         per % 128 == 0
         and per & (per - 1) == 0
         and rows % 128 == 0
         and width % 128 == 0
         and n // 2 * cap % 128 == 0
-        and n // cols * spill % 128 == 0
-        and n // cols * (spill * 3 // 2) % 64 == 0
+        and spill % 8 == 0
         and cols == 8
         and n == 4 * cols
         and n <= 128
-        and 2 * cap + spill * 3 // 2 < EXTRA - 1
+        and 2 * cap + 2 * spill < EXTRA - 1
     )
     if fits:
         return asked_plan(n, cols, cap, spill, tokens, codebook, codes)

time: 29 us -> 27.7 us (0.955)
  Pallas kernels: 27 us -> 25.8 us
    pallas_call x1, Pallas kernels: 25.6 us -> 24.5 us  [exchange(): pl.pallas_call(functools.partial(kernel, n, cols, cap, spill, wide_spill)...]
where the time goes in v4:
time: 27.7 us; the launch traced here: 27.6 us
  Pallas kernels  25.8 us (93%)
  between operations  1.51 us (5%)
    pallas_call x1, Pallas kernels, exchange(): pl.pallas_call(functools.partial(kernel, n, cols, cap, spill, wide_spill)...  24.5 us
    pallas_call x1, Pallas kernels, finish(): pl.pallas_call(finish_kernel, out_shape=(jax.ShapeDtypeStruct(quantized.s...  1.35 us

profile of v4, /device:TPU:0, one launch (start us, length us, event | category | flops | bytes accessed | tf_op | source)
XLA Modules:
  0.0 27.6 jit_solution(9520748477006259700)
XLA Ops:
  0.6 0.0 copy-start
  0.6 24.5 %shard_map.86 = (bf16[768,256]{1,0:T(8,128)(2,1)S(1)}, f32[1,768]{1,0:T(1,128)S(1)}, s32[1,512]{1,0:T(1,128)S(1)}, f32[1,512]{1,0:T(1,128)S(1)}, f32[1,128]{1,0:T(1,128)S(1)}) custom-call(s32[768]{0:T(1024)} %codes_hbm.1, bf16[768,256]{1,0:T(8,128)(2,1)} %tokens_hbm.1, bf16[512,256]{1,0:T(8,128)(2,1)} %book_hbm.1), custom_call_target="tpu_custom_call" | custom-call | tf_op jit(solution)/shard_map/pallas_call | solution.py:404
  25.1 0.0 copy-start.2
  25.1 1.4 %shard_map.87 = (bf16[768,256]{1,0:T(8,128)(2,1)}, f32[768]{0:T(1024)}, s32[512]{0:T(512)}, f32[512]{0:T(512)}, f32[1,1]{1,0:T(1,128)}, /*index=5*/f32[1,1]{1,0:T(1,128)}, s32[1,1]{1,0:T(1,128)}) custom-call(bf16[768,256]{1,0:T(8,128)(2,1)S(1)} %get-tuple-element.454.quant_ref, f32[1,768]{1,0:T(1,128)S(1)} %get-tuple-element.455.tloss_ref, ...), custom_call_target="tpu_custom_call" | custom-call | tf_op jit(solution)/shard_map/pallas_call | solution.py:464
  26.5 0.0 copy-start.4
  27.1 0.0 copy-done
  27.1 0.0 copy-done.2
  27.2 0.0 copy-done.4
  27.2 0.2 conditional.2
Async XLA Ops:
  0.6 26.5 %copy-start = (bf16[768,256]{1,0:T(8,128)(2,1)S(1)}, bf16[768,256]{1,0:T(8,128)(2,1)}, u32[]{:S(2)}) copy-start(bf16[768,256]{1,0:T(8,128)(2,1)} %tokens_hbm.1) | copy-start | bytes 1179652
  25.1 2.0 %copy-start.2 = (bf16[512,256]{1,0:T(8,128)(2,1)S(1)}, bf16[512,256]{1,0:T(8,128)(2,1)}, u32[]{:S(2)}) copy-start(bf16[512,256]{1,0:T(8,128)(2,1)} %book_hbm.1) | copy-start | bytes 786436
  26.5 0.7 %copy-start.4 = (s32[768]{0:T(1024)S(1)}, s32[768]{0:T(1024)}, u32[]{:S(2)}) copy-start(s32[768]{0:T(1024)} %codes_hbm.1) | copy-start | bytes 9220

commit v5 on v4

--- a/solution.py
+++ b/solution.py
@@ -57,8 +57,6 @@
     per_dev = codebook.shape[0]
     me = lax.axis_index(AXES)
     ring = [(i, (i + 1) % n) for i in range(n)]
-    codes = jnp.where(me < n, codes, 0)
-    codebook = jnp.where(me < n, codebook, 0)
     hi = codes // per_dev
     lo = codes % per_dev
 
@@ -445,22 +443,30 @@
 
 def finish_kernel(
     quant_ref, tloss_ref, counts_ref, closs_ref, scal_ref,
-    quant_out, tloss_out, counts_out, closs_out, commit_out, perp_out, flag_out, sem,
+    quant_out, tloss_out, counts_out, closs_out, commit_out, perp_out, flag_out,
+    tloss, counts, closs, commit, perp, sem,
 ):
-    put = pltpu.make_async_copy(quant_ref, quant_out, sem)
-    put.start()
-    tloss_out[...] = tloss_ref[...].reshape(tloss_out.shape)
-    counts_out[...] = counts_ref[...].reshape(counts_out.shape)
-    closs_out[...] = closs_ref[...].reshape(closs_out.shape)
-    commit_out[...] = scal_ref[:, :1]
-    perp_out[...] = scal_ref[:, 1:2]
-    flag_out[...] = scal_ref[:, 2:3].astype(jnp.int32)
-    put.wait()
+    whole = pltpu.make_async_copy(quant_ref, quant_out, sem.at[0])
+    whole.start()
+    tloss[...] = tloss_ref[...].reshape(tloss.shape)
+    counts[...] = counts_ref[...].reshape(counts.shape)
+    closs[...] = closs_ref[...].reshape(closs.shape)
+    commit[...] = scal_ref[:, :1]
+    perp[...] = scal_ref[:, 1:2]
+    small = [(tloss, tloss_out), (counts, counts_out), (closs, closs_out), (commit, commit_out), (perp, perp_out)]
+    small = [pltpu.make_async_copy(src, dst, sem.at[1 + i]) for i, (src, dst) in enumerate(small)]
+    for one in small:
+        one.start()
+    flag_out[0, 0] = jnp.max(scal_ref[:, 2:3]).astype(jnp.int32)
+    for one in small:
+        one.wait()
+    whole.wait()
 
 
 def finish(quantized, token_loss, counts, code_loss, scalars):
     rows, per = token_loss.shape[1], counts.shape[1]
     vmem = pl.BlockSpec(memory_space=pltpu.VMEM)
+    hbm = pl.BlockSpec(memory_space=pltpu.HBM)
     q, t, k, c, m, p, f = pl.pallas_call(
         finish_kernel,
         out_shape=(
@@ -470,16 +476,38 @@
             jax.ShapeDtypeStruct((per,), F32),
             jax.ShapeDtypeStruct((1, 1), F32),
             jax.ShapeDtypeStruct((1, 1), F32),
-            jax.ShapeDtypeStruct((1, 1), jnp.int32),
+            pltpu.SMEM((1, 1), jnp.int32),
         ),
         in_specs=[vmem] * 5,
-        out_specs=(pl.BlockSpec(memory_space=pltpu.HBM), vmem, vmem, vmem, vmem, vmem, vmem),
-        scratch_shapes=[pltpu.SemaphoreType.DMA],
+        out_specs=(hbm,) * 6 + (pl.BlockSpec(memory_space=pltpu.SMEM),),
+        scratch_shapes=[
+            pltpu.VMEM((rows,), F32),
+            pltpu.VMEM((per,), jnp.int32),
+            pltpu.VMEM((per,), F32),
+            pltpu.VMEM((1, 1), F32),
+            pltpu.VMEM((1, 1), F32),
+            pltpu.SemaphoreType.DMA((6,)),
+        ],
         compiler_params=pltpu.CompilerParams(vmem_limit_bytes=4 << 20),
     )(quantized, token_loss, counts, code_loss, scalars)
     return q, t, k, c, m[0, 0], p[0, 0], f
 
 
+def held(x):
+    def body(src, dst, sem):
+        copy = pltpu.make_async_copy(src, dst, sem)
+        copy.start()
+        copy.wait()
+
+    return pl.pallas_call(
+        body,
+        out_shape=jax.ShapeDtypeStruct(x.shape, x.dtype),
+        in_specs=[pl.BlockSpec(memory_space=pltpu.HBM)],
+        out_specs=pl.BlockSpec(memory_space=pltpu.VMEM),
+        scratch_shapes=[pltpu.SemaphoreType.DMA],
+    )(pltpu.with_memory_space_constraint(x, pltpu.HBM))
+
+
 def asked_plan(n, cols, cap, spill, tokens, codebook, codes):
     wide = spill * 2
     outs = exchange(n, cols, cap, spill, wide, 0, tokens, codebook, codes)
@@ -493,7 +521,7 @@
         return finish(*exchange(n, cols, 2 * cap, wide, wide, 1, tokens, codebook, codes))[:-1]
 
     def ringed():
-        return ring_plan(n, tokens, codebook, codes)
+        return ring_plan(n, held(tokens), held(codebook), held(codes))
 
     def any_codes():
         return lax.cond(flag[0, 0] > 1, ringed, wider)

time: 27.7 us -> 26.5 us (0.957)
  between operations: 1.51 us -> 0.83 us
  Pallas kernels: 25.8 us -> 25.3 us
    pallas_call x1, Pallas kernels: 1.35 us -> 0.8 us  [finish(): pl.pallas_call(finish_kernel, out_shape=(jax.ShapeDtypeStruct(quantized.s...]
where the time goes in v5:
time: 26.5 us; the launch traced here: 26.3 us
  Pallas kernels  25.3 us (95%)
  between operations  0.83 us (3%)
    pallas_call x1, Pallas kernels, exchange(): pl.pallas_call(functools.partial(kernel, n, cols, cap, spill, wide_spill)...  24.5 us
    pallas_call x1, Pallas kernels, finish(): pl.pallas_call(finish_kernel, out_shape=(jax.ShapeDtypeStruct(quantized.s...  0.8 us

profile of v5, /device:TPU:0, one launch (start us, length us, event | category | flops | bytes accessed | tf_op | source)
XLA Modules:
  0.0 26.3 jit_solution(17972460736867189246)
XLA Ops:
  0.6 24.5 %shard_map.86 = (bf16[768,256]{1,0:T(8,128)(2,1)S(1)}, f32[1,768]{1,0:T(1,128)S(1)}, s32[1,512]{1,0:T(1,128)S(1)}, f32[1,512]{1,0:T(1,128)S(1)}, f32[1,128]{1,0:T(1,128)S(1)}) custom-call(s32[768]{0:T(1024)} %codes_hbm.1, bf16[768,256]{1,0:T(8,128)(2,1)} %tokens_hbm.1, bf16[512,256]{1,0:T(8,128)(2,1)} %book_hbm.1), custom_call_target="tpu_custom_call" | custom-call | tf_op jit(solution)/shard_map/pallas_call | solution.py:402
  25.1 0.8 %shard_map.87 = (bf16[768,256]{1,0:T(8,128)(2,1)}, f32[768]{0:T(1024)}, s32[512]{0:T(512)}, f32[512]{0:T(512)}, f32[1,1]{1,0:T(1,128)}, /*index=5*/f32[1,1]{1,0:T(1,128)}, s32[1,1]{1,0:T(1,128)S(4)}) custom-call(bf16[768,256]{1,0:T(8,128)(2,1)S(1)} %get-tuple-element.454.quant_ref, f32[1,768]{1,0:T(1,128)S(1)} %get-tuple-element.455.tloss_ref, ...), custom_call_target="tpu_custom_call" | custom-call | tf_op jit(solution)/shard_map/pallas_call | solution.py:470
  25.9 0.2 conditional.2

commit v6 on v5

--- a/solution.py
+++ b/solution.py
@@ -108,7 +108,7 @@
     codes_hbm, tokens_hbm, book_hbm,
     quant_ref, tloss_ref, counts_ref, closs_ref, scal_ref,
     codes_ref, tokens_ref, book_ref, csend, crecv, hsend, hrecv, psend, precv, gsend, grecv, osend, orecv,
-    dsend, drecv, lsend, lrecv, low1h, sel, spill1h, rank1h,
+    dsend, drecv, lsend, lrecv, low1h, sel, spill1h, rank1h, direct,
     in_sem, csem_s, csem_r, hsem_s, hsem_r, psem_s, psem_r,
     gsem_s, gsem_r, osem_s, osem_r, lsem_s, lsem_r, bsem, dsem,
 ):
@@ -265,7 +265,8 @@
         spill1h[:, k : k + wide] = jnp.where(slot == lane + k, 1.0, 0.0).astype(BF16)[:, :wide]
 
     both_caps = cap + -(-spill // 16) * 16
-    place = lax.broadcasted_iota(jnp.int32, (both_caps, per), 0).astype(F32)
+    place = lax.broadcasted_iota(jnp.int32, (both_caps, per), 0).astype(F32).astype(BF16)
+    one, none = jnp.ones((), BF16), jnp.zeros((), BF16)
     for i, d in enumerate(REPLY_ORDER):
         group = range(d * half, d * half + half)
         all_in(crecv, half if d else half - 1, csem_r.at[rows_at[d]])
@@ -276,7 +277,7 @@
             pair = crecv[peer[k]][:, :per].astype(F32)
             picks.append(jnp.concatenate(
                 [
-                    jnp.where(jnp.broadcast_to(pair[h : h + 1], (both_caps, per)) == place, 1.0, 0.0).astype(BF16)
+                    jnp.where(jnp.broadcast_to(pair[h : h + 1], (both_caps, per)).astype(BF16) == place, one, none)
                     for h in (0, 1)
                 ],
                 axis=1,
@@ -335,10 +336,10 @@
     all_in(precv, chips - 1, psem_r)
     fetch_tokens.wait()
     packs = precv[...].reshape(chips * cap, width)
-    direct = jnp.dot(sel[...], packs, preferred_element_type=F32)
+    direct[...] = jnp.dot(sel[...], packs, preferred_element_type=F32)
     all_in(orecv, planes - 1, osem_r)
     packs = orecv[...].reshape(planes * spill, width)
-    quant = (direct + jnp.dot(spill1h[...], packs, preferred_element_type=F32)).astype(BF16)
+    quant = (direct[...] + jnp.dot(spill1h[...], packs, preferred_element_type=F32)).astype(BF16)
     quant_ref[...] = quant
     diff = tokens_ref[...].astype(F32) - quant.astype(F32)
     square = diff * diff
@@ -432,6 +433,7 @@
             pltpu.VMEM((rows, chips * cap), BF16),
             pltpu.VMEM((rows, planes * spill), BF16),
             pltpu.VMEM((rows, 128), BF16),
+            pltpu.VMEM((rows, width), F32),
             dma((3,)),
             dma, dma((planes,)), *[dma] * 4,
             dma, dma((planes,)), *[dma] * 4,

time: 26.5 us -> 26.1 us (0.985)
  Pallas kernels: 25.3 us -> 24.9 us
    pallas_call x1, Pallas kernels: 24.5 us -> 24.1 us  [exchange(): pl.pallas_call(functools.partial(kernel, n, cols, cap, spill, wide_spill)...]
where the time goes in v6:
time: 26.1 us; the launch traced here: 25.9 us
  Pallas kernels  24.9 us (95%)
  between operations  0.83 us (3%)
    pallas_call x1, Pallas kernels, exchange(): pl.pallas_call(functools.partial(kernel, n, cols, cap, spill, wide_spill)...  24.1 us
    pallas_call x1, Pallas kernels, finish(): pl.pallas_call(finish_kernel, out_shape=(jax.ShapeDtypeStruct(quantized.s...  0.8 us

profile of v6, /device:TPU:0, one launch (start us, length us, event | category | flops | bytes accessed | tf_op | source)
XLA Modules:
  0.0 25.9 jit_solution(6046802686101284168)
XLA Ops:
  0.6 24.1 %shard_map.86 = (bf16[768,256]{1,0:T(8,128)(2,1)S(1)}, f32[1,768]{1,0:T(1,128)S(1)}, s32[1,512]{1,0:T(1,128)S(1)}, f32[1,512]{1,0:T(1,128)S(1)}, f32[1,128]{1,0:T(1,128)S(1)}) custom-call(s32[768]{0:T(1024)} %codes_hbm.1, bf16[768,256]{1,0:T(8,128)(2,1)} %tokens_hbm.1, bf16[512,256]{1,0:T(8,128)(2,1)} %book_hbm.1), custom_call_target="tpu_custom_call" | custom-call | tf_op jit(solution)/shard_map/pallas_call | solution.py:403
  24.7 0.8 %shard_map.87 = (bf16[768,256]{1,0:T(8,128)(2,1)}, f32[768]{0:T(1024)}, s32[512]{0:T(512)}, f32[512]{0:T(512)}, f32[1,1]{1,0:T(1,128)}, /*index=5*/f32[1,1]{1,0:T(1,128)}, s32[1,1]{1,0:T(1,128)S(4)}) custom-call(bf16[768,256]{1,0:T(8,128)(2,1)S(1)} %get-tuple-element.454.quant_ref, f32[1,768]{1,0:T(1,128)S(1)} %get-tuple-element.455.tloss_ref, ...), custom_call_target="tpu_custom_call" | custom-call | tf_op jit(solution)/shard_map/pallas_call | solution.py:472
  25.5 0.2 conditional.2

commit v7 on v6

--- a/solution.py
+++ b/solution.py
@@ -9,7 +9,7 @@
 
 AXES = ("row", "col")
 EXTRA = 128
-ASK_ORDER = (3, 2, 1, 0)
+ASK_ORDER = (2, 3, 1, 0)
 REPLY_ORDER = (2, 3, 1, 0)
 F32 = jnp.float32
 BF16 = jnp.bfloat16
@@ -232,8 +232,7 @@
     rank = jnp.minimum(rank + jnp.where(rank > cap - 0.5, behind, 0.0), 255.0)
     order = jnp.where(wanted > 0.5, rank, -1.0).astype(BF16)
     for q in range(chips):
-        csend[q, :, :per] = order[2 * q : 2 * q + 2, :]
-        csend[q, :, per:] = most_pair
+        csend[q] = order[2 * q : 2 * q + 2, :]
     crecv[pl.ds(me, 1)] = csend[pl.ds(me, 1)]
 
     pl.semaphore_wait(barrier, n - 1)
@@ -241,7 +240,8 @@
         put(*ask_refs, k).start()
     hist16 = jnp.minimum(hist, 256.0).astype(BF16)
     for q in range(chips):
-        hsend[q] = hist16[2 * q : 2 * q + 2, :]
+        hsend[q, :, :per] = hist16[2 * q : 2 * q + 2, :]
+        hsend[q, :, per:] = most_pair
     hrecv[pl.ds(me, 1)] = hsend[pl.ds(me, 1)]
     fetch_book.wait()
     share_book.start()
@@ -274,7 +274,7 @@
             share_book.wait_recv()
         picks = []
         for k in group:
-            pair = crecv[peer[k]][:, :per].astype(F32)
+            pair = crecv[peer[k]].astype(F32)
             picks.append(jnp.concatenate(
                 [
                     jnp.where(jnp.broadcast_to(pair[h : h + 1], (both_caps, per)).astype(BF16) == place, one, none)
@@ -316,9 +316,9 @@
     side = jnp.where(turn < chips, core, 1 - core)
     which = 2 * lax.rem(turn, chips) + side
     split = jnp.where(lax.broadcasted_iota(jnp.int32, (n, n), 1) == which, 1.0, 0.0).astype(BF16)
-    both = jnp.concatenate([got[:, :per].astype(BF16), asked.astype(BF16)], axis=1)
+    both = jnp.concatenate([got.astype(BF16), asked[:, :per].astype(BF16)], axis=1)
     both = jnp.dot(split, both, preferred_element_type=F32)
-    most_asked = jnp.max(got[:, per:], axis=0, keepdims=True)
+    most_asked = jnp.max(asked[:, per:], axis=0, keepdims=True)
     dsend[:, : 2 * per] = both[chips:]
     dsend[:, 2 * per :] = jnp.broadcast_to(most_asked, (chips, EXTRA))
     share_asks.start()
@@ -415,10 +415,10 @@
             pltpu.VMEM(codes.shape, jnp.int32),
             pltpu.VMEM((rows, width), BF16),
             pltpu.VMEM((2 * per, width), BF16),
+            pltpu.VMEM((chips, 2, per), BF16),
+            pltpu.VMEM((chips, 2, per), BF16),
             pltpu.VMEM((chips, 2, per + EXTRA), BF16),
             pltpu.VMEM((chips, 2, per + EXTRA), BF16),
-            pltpu.VMEM((chips, 2, per), BF16),
-            pltpu.VMEM((chips, 2, per), BF16),
             pltpu.VMEM((chips, cap, width), BF16),
             pltpu.VMEM((chips, cap, width), BF16),
             pltpu.VMEM((planes, cols // 2, spill, width), BF16),

time: 26.1 us -> 26 us (level)
  no operation moved by 1% of the time
where the time goes in v7:
time: 26 us; the launch traced here: 25.8 us
  Pallas kernels  24.7 us (95%)
  between operations  0.83 us (3%)
    pallas_call x1, Pallas kernels, exchange(): pl.pallas_call(functools.partial(kernel, n, cols, cap, spill, wide_spill)...  23.9 us
    pallas_call x1, Pallas kernels, finish(): pl.pallas_call(finish_kernel, out_shape=(jax.ShapeDtypeStruct(quantized.s...  0.8 us

profile of v7, /device:TPU:0, one launch (start us, length us, event | category | flops | bytes accessed | tf_op | source)
XLA Modules:
  0.0 25.8 jit_solution(10197249431234868307)
XLA Ops:
  0.6 23.9 %shard_map.86 = (bf16[768,256]{1,0:T(8,128)(2,1)S(1)}, f32[1,768]{1,0:T(1,128)S(1)}, s32[1,512]{1,0:T(1,128)S(1)}, f32[1,512]{1,0:T(1,128)S(1)}, f32[1,128]{1,0:T(1,128)S(1)}) custom-call(s32[768]{0:T(1024)} %codes_hbm.1, bf16[768,256]{1,0:T(8,128)(2,1)} %tokens_hbm.1, bf16[512,256]{1,0:T(8,128)(2,1)} %book_hbm.1), custom_call_target="tpu_custom_call" | custom-call | tf_op jit(solution)/shard_map/pallas_call | solution.py:403
  24.6 0.8 %shard_map.87 = (bf16[768,256]{1,0:T(8,128)(2,1)}, f32[768]{0:T(1024)}, s32[512]{0:T(512)}, f32[512]{0:T(512)}, f32[1,1]{1,0:T(1,128)}, /*index=5*/f32[1,1]{1,0:T(1,128)}, s32[1,1]{1,0:T(1,128)S(4)}) custom-call(bf16[768,256]{1,0:T(8,128)(2,1)S(1)} %get-tuple-element.454.quant_ref, f32[1,768]{1,0:T(1,128)S(1)} %get-tuple-element.455.tloss_ref, ...), custom_call_target="tpu_custom_call" | custom-call | tf_op jit(solution)/shard_map/pallas_call | solution.py:472
  25.4 0.2 conditional.2

commit v8 on v7

--- a/solution.py
+++ b/solution.py
@@ -123,9 +123,13 @@
     me = my_row * half + my_chip
     inner = lax.rem(lax.div(my_row + 1, 2), 2)
     beside, across = my_row + 1 - 2 * lax.rem(my_row, 2), 3 - my_row
+    skip, late = lax.rem(my_row + 2, 4), lax.div(my_row, 2)
     near = inner * across + (1 - inner) * beside
     far = inner * beside + (1 - inner) * across
-    rows_at = [my_row, near, lax.rem(my_row + 2, 4), far]
+    first = late * beside + (1 - late) * skip
+    then = late * skip + (1 - late) * far
+    last = late * across + (1 - late) * near
+    rows_at = [my_row, last, first, then]
     chips_at = [
         my_chip, my_chip + 1 - 2 * lax.rem(my_chip, 2), lax.rem(my_chip + 2, 4), 3 - my_chip
     ]
@@ -272,31 +276,32 @@
         all_in(crecv, half if d else half - 1, csem_r.at[rows_at[d]])
         if i == 0:
             share_book.wait_recv()
-        picks = []
-        for k in group:
-            pair = crecv[peer[k]].astype(F32)
-            picks.append(jnp.concatenate(
-                [
-                    jnp.where(jnp.broadcast_to(pair[h : h + 1], (both_caps, per)).astype(BF16) == place, one, none)
-                    for h in (0, 1)
-                ],
-                axis=1,
-            ))
-        packed = jnp.dot(jnp.concatenate(picks, axis=0), book_ref[...], preferred_element_type=F32)
-        packed = packed.astype(BF16)
-        for j, k in enumerate(group):
-            out = psend if k else precv
-            start = j * both_caps
-            out[peer[k]] = packed[start : start + cap]
-            if j:
-                gsend[rows_at[d], chips_at[j]] = packed[start + cap : start + cap + spill]
-            else:
-                grecv[rows_at[d], my_chip] = packed[start + cap : start + cap + spill]
-        for c in range(1, half):
-            spill_put(d, c).start()
-        for k in group:
-            if k:
-                put(*reply_refs, k).start()
+        for first in range(0, half, 2):
+            picks = []
+            for k in group[first : first + 2]:
+                pair = crecv[peer[k]].astype(F32)
+                picks.append(jnp.concatenate(
+                    [
+                        jnp.where(jnp.broadcast_to(pair[h : h + 1], (both_caps, per)).astype(BF16) == place, one, none)
+                        for h in (0, 1)
+                    ],
+                    axis=1,
+                ))
+            packed = jnp.dot(jnp.concatenate(picks, axis=0), book_ref[...], preferred_element_type=F32)
+            packed = packed.astype(BF16)
+            for j, k in enumerate(group[first : first + 2]):
+                c = first + j
+                out = psend if k else precv
+                start = j * both_caps
+                out[peer[k]] = packed[start : start + cap]
+                if c:
+                    gsend[rows_at[d], chips_at[c]] = packed[start + cap : start + cap + spill]
+                    spill_put(d, c).start()
+                else:
+                    grecv[rows_at[d], my_chip] = packed[start + cap : start + cap + spill]
+            for k in group[first : first + 2]:
+                if k:
+                    put(*reply_refs, k).start()
 
     for d in REPLY_ORDER:
         all_in(grecv.at[0], half - 1, gsem_r.at[rows_at[d]])

time: 26 us -> 25.7 us (0.988)
  Pallas kernels: 24.7 us -> 24.4 us
    pallas_call x1, Pallas kernels: 23.9 us -> 23.6 us  [exchange(): pl.pallas_call(functools.partial(kernel, n, cols, cap, spill, wide_spill)...]
where the time goes in v8:
time: 25.7 us; the launch traced here: 25.5 us
  Pallas kernels  24.4 us (95%)
  between operations  0.83 us (3%)
    pallas_call x1, Pallas kernels, exchange(): pl.pallas_call(functools.partial(kernel, n, cols, cap, spill, wide_spill)...  23.6 us
    pallas_call x1, Pallas kernels, finish(): pl.pallas_call(finish_kernel, out_shape=(jax.ShapeDtypeStruct(quantized.s...  0.8 us

profile of v8, /device:TPU:0, one launch (start us, length us, event | category | flops | bytes accessed | tf_op | source)
XLA Modules:
  0.0 25.5 jit_solution(2662385231080803598)
XLA Ops:
  0.6 23.6 %shard_map.86 = (bf16[768,256]{1,0:T(8,128)(2,1)S(1)}, f32[1,768]{1,0:T(1,128)S(1)}, s32[1,512]{1,0:T(1,128)S(1)}, f32[1,512]{1,0:T(1,128)S(1)}, f32[1,128]{1,0:T(1,128)S(1)}) custom-call(s32[768]{0:T(1024)} %codes_hbm.1, bf16[768,256]{1,0:T(8,128)(2,1)} %tokens_hbm.1, bf16[512,256]{1,0:T(8,128)(2,1)} %book_hbm.1), custom_call_target="tpu_custom_call" | custom-call | tf_op jit(solution)/shard_map/pallas_call | solution.py:408
  24.3 0.8 %shard_map.87 = (bf16[768,256]{1,0:T(8,128)(2,1)}, f32[768]{0:T(1024)}, s32[512]{0:T(512)}, f32[512]{0:T(512)}, f32[1,1]{1,0:T(1,128)}, /*index=5*/f32[1,1]{1,0:T(1,128)}, s32[1,1]{1,0:T(1,128)S(4)}) custom-call(bf16[768,256]{1,0:T(8,128)(2,1)S(1)} %get-tuple-element.454.quant_ref, f32[1,768]{1,0:T(1,128)S(1)} %get-tuple-element.455.tloss_ref, ...), custom_call_target="tpu_custom_call" | custom-call | tf_op jit(solution)/shard_map/pallas_call | solution.py:477
  25.1 0.2 conditional.2

commit v9 on v8

--- a/solution.py
+++ b/solution.py
@@ -276,9 +276,10 @@
         all_in(crecv, half if d else half - 1, csem_r.at[rows_at[d]])
         if i == 0:
             share_book.wait_recv()
-        for first in range(0, half, 2):
+        step = half if i else 2
+        for first in range(0, half, step):
             picks = []
-            for k in group[first : first + 2]:
+            for k in group[first : first + step]:
                 pair = crecv[peer[k]].astype(F32)
                 picks.append(jnp.concatenate(
                     [
@@ -289,7 +290,7 @@
                 ))
             packed = jnp.dot(jnp.concatenate(picks, axis=0), book_ref[...], preferred_element_type=F32)
             packed = packed.astype(BF16)
-            for j, k in enumerate(group[first : first + 2]):
+            for j, k in enumerate(group[first : first + step]):
                 c = first + j
                 out = psend if k else precv
                 start = j * both_caps
@@ -299,7 +300,7 @@
                     spill_put(d, c).start()
                 else:
                     grecv[rows_at[d], my_chip] = packed[start + cap : start + cap + spill]
-            for k in group[first : first + 2]:
+            for k in group[first : first + step]:
                 if k:
                     put(*reply_refs, k).start()
 

time: 25.7 us -> 26.1 us (1.016)
  Pallas kernels: 24.4 us -> 24.9 us
    pallas_call x1, Pallas kernels: 23.6 us -> 24.1 us  [exchange(): pl.pallas_call(functools.partial(kernel, n, cols, cap, spill, wide_spill)...]
where the time goes in v9:
time: 26.1 us; the launch traced here: 25.9 us
  Pallas kernels  24.9 us (95%)
  between operations  0.83 us (3%)
    pallas_call x1, Pallas kernels, exchange(): pl.pallas_call(functools.partial(kernel, n, cols, cap, spill, wide_spill)...  24.1 us
    pallas_call x1, Pallas kernels, finish(): pl.pallas_call(finish_kernel, out_shape=(jax.ShapeDtypeStruct(quantized.s...  0.8 us

profile of v9, /device:TPU:0, one launch (start us, length us, event | category | flops | bytes accessed | tf_op | source)
XLA Modules:
  0.0 25.9 jit_solution(318825066855397460)
XLA Ops:
  0.6 24.1 %shard_map.86 = (bf16[768,256]{1,0:T(8,128)(2,1)S(1)}, f32[1,768]{1,0:T(1,128)S(1)}, s32[1,512]{1,0:T(1,128)S(1)}, f32[1,512]{1,0:T(1,128)S(1)}, f32[1,128]{1,0:T(1,128)S(1)}) custom-call(s32[768]{0:T(1024)} %codes_hbm.1, bf16[768,256]{1,0:T(8,128)(2,1)} %tokens_hbm.1, bf16[512,256]{1,0:T(8,128)(2,1)} %book_hbm.1), custom_call_target="tpu_custom_call" | custom-call | tf_op jit(solution)/shard_map/pallas_call | solution.py:409
  24.7 0.8 %shard_map.87 = (bf16[768,256]{1,0:T(8,128)(2,1)}, f32[768]{0:T(1024)}, s32[512]{0:T(512)}, f32[512]{0:T(512)}, f32[1,1]{1,0:T(1,128)}, /*index=5*/f32[1,1]{1,0:T(1,128)}, s32[1,1]{1,0:T(1,128)S(4)}) custom-call(bf16[768,256]{1,0:T(8,128)(2,1)S(1)} %get-tuple-element.454.quant_ref, f32[1,768]{1,0:T(1,128)S(1)} %get-tuple-element.455.tloss_ref, ...), custom_call_target="tpu_custom_call" | custom-call | tf_op jit(solution)/shard_map/pallas_call | solution.py:478
  25.5 0.2 conditional.2
